TPU v7x, 32 devices: a 4x4x1 block of a 4x4x8 slice. The times are simulated.
32 devices in a mesh: dp: 1 (over z), cp: 32 (over y, x, core).
Axes of the slice: x: 4, y: 4, z: 1, core: 2. Of those that a mesh axis runs over, the one named last changes fastest.
The devices are a block of a 4x4x8 slice.
Arguments:
- hidden: bfloat16 [6, 3072, 3584], P('dp', 'cp')
- positions: int32 [6, 3072], P('dp', 'cp')
- w_q: bfloat16 [3584, 16, 256], replicated
- w_k: bfloat16 [3584, 8, 256], replicated
- w_v: bfloat16 [3584, 8, 256], replicated
- w_o: bfloat16 [16, 256, 3584], replicated
Outputs:
- output: bfloat16 [6, 3072, 3584], P('dp', 'cp')
All inputs are finite; a program needn't handle non-finite values.
Results may differ from a plain program's by a relative error of at most 0.00861.
Values are sent between devices in bfloat16 or wider.
A program may use at most 768 MiB of HBM per device.

v0:
```python
import jax
import jax.numpy as jnp
from jax import lax
from jax.sharding import PartitionSpec as P

ROPE_BASE = 500000.0


def rope_tables(positions, head_dim):
    inv_freq = ROPE_BASE ** (-jnp.arange(0, head_dim, 2, dtype=jnp.float32) / head_dim)
    angles = positions.astype(jnp.float32)[..., None] * inv_freq
    angles = jnp.concatenate([angles, angles], axis=-1)
    return jnp.cos(angles)[:, :, None, :], jnp.sin(angles)[:, :, None, :]


def rope_apply(in_vals, cos_tab, sin_tab):
    half_dim = in_vals.shape[-1] // 2
    val_f32 = in_vals.astype(jnp.float32)
    rotated = jnp.concatenate([-val_f32[..., half_dim:], val_f32[..., :half_dim]], axis=-1)
    return (val_f32 * cos_tab + rotated * sin_tab).astype(jnp.bfloat16)


def project_qkv(hidden, positions, w_q, w_k, w_v):
    n_batch, tok_len = hidden.shape[0], hidden.shape[1]
    n_kv, head_dim = w_k.shape[1], w_k.shape[2]
    q_per_kv = w_q.shape[1] // n_kv
    queries = jnp.einsum('bsd,dhe->bshe', hidden, w_q, preferred_element_type=jnp.float32).astype(jnp.bfloat16)
    k_proj = jnp.einsum('bsd,dhe->bshe', hidden, w_k, preferred_element_type=jnp.float32).astype(jnp.bfloat16)
    values = jnp.einsum('bsd,dhe->bshe', hidden, w_v, preferred_element_type=jnp.float32).astype(jnp.bfloat16)
    cos_tab, sin_tab = rope_tables(positions, head_dim)
    queries = rope_apply(queries, cos_tab, sin_tab).reshape(n_batch, tok_len, n_kv, q_per_kv, head_dim)
    k_rot = rope_apply(k_proj, cos_tab, sin_tab)
    return queries, k_rot, values


def empty_state(queries):
    n_batch, tok_len, n_kv, q_per_kv, head_dim = queries.shape
    run_max = jnp.full((n_batch, n_kv, q_per_kv, tok_len), -jnp.inf, jnp.float32)
    run_sum = jnp.zeros((n_batch, n_kv, q_per_kv, tok_len), jnp.float32)
    out_acc = jnp.zeros((n_batch, n_kv, q_per_kv, tok_len, head_dim), jnp.float32)
    return run_max, run_sum, out_acc


def block_update(sm_state, queries, k_blk, v_blk, allowed):
    run_max, run_sum, out_acc = sm_state
    sm_scale = queries.shape[-1] ** -0.5
    scores = jnp.einsum('bqkge,bske->bkgqs', queries, k_blk, preferred_element_type=jnp.float32) * sm_scale
    scores = jnp.where(allowed, scores, -jnp.inf)
    new_max = jnp.maximum(run_max, jnp.max(scores, axis=-1))
    correction = jnp.exp(run_max - new_max)
    p_weights = jnp.exp(scores - new_max[..., None])
    run_sum = run_sum * correction + jnp.sum(p_weights, axis=-1)
    pv_part = jnp.einsum('bkgqs,bske->bkgqe', p_weights.astype(jnp.bfloat16), v_blk, preferred_element_type=jnp.float32)
    out_acc = out_acc * correction[..., None] + pv_part
    return new_max, run_sum, out_acc


def finish(sm_state, hidden, w_o):
    run_sum, out_acc = sm_state[1], sm_state[2]
    n_kv, q_per_kv, head_dim = out_acc.shape[1], out_acc.shape[2], out_acc.shape[4]
    attn_out = (out_acc / run_sum[..., None]).astype(jnp.bfloat16)
    w_o_grp = w_o.reshape(n_kv, q_per_kv, head_dim, w_o.shape[2])
    proj_out = jnp.einsum('clhrf,lhfe->cre', attn_out, w_o_grp, preferred_element_type=jnp.float32)
    return (hidden.astype(jnp.float32) + proj_out).astype(jnp.bfloat16)


def solution(mesh):
    cp_size = mesh.shape['cp']
    shift_pairs = [(j, (j + 1) % cp_size) for j in range(cp_size)]

    def per_device(hidden, positions, w_q, w_k, w_v, w_o):
        queries, k_rot, values = project_qkv(hidden, positions, w_q, w_k, w_v)
        tok_dev = hidden.shape[1]
        my_idx = lax.axis_index('cp')
        row_ids = jnp.arange(tok_dev)[:, None]
        col_ids = jnp.arange(tok_dev)[None, :]
        sm_state = block_update(empty_state(queries), queries, k_rot, values, col_ids <= row_ids)

        def kv_step(step_idx, loop_vals):
            cur_state, k_cur, v_cur = loop_vals
            k_cur = lax.ppermute(k_cur, 'cp', shift_pairs)
            v_cur = lax.ppermute(v_cur, 'cp', shift_pairs)
            src_idx = (my_idx - step_idx) % cp_size
            cur_state = block_update(cur_state, queries, k_cur, v_cur, src_idx < my_idx)
            return cur_state, k_cur, v_cur

        sm_state, k_last, v_last = lax.fori_loop(1, cp_size, kv_step, (sm_state, k_rot, values))
        return finish(sm_state, hidden, w_o)

    rep_spec = P(None, None, None)
    return jax.shard_map(per_device, mesh=mesh, in_specs=(P('dp', 'cp', None), P('dp', 'cp'), rep_spec, rep_spec, rep_spec, rep_spec), out_specs=P('dp', 'cp', None), check_vma=False)
```

profile of v0, /device:TPU:96, one launch (start us, length us, event | category | flops | bytes accessed | tf_op | source)
XLA Modules:
  0.0 2142.7 jit_solution(16593725994417544638)
XLA Ops:
  19.5 21.1 convert_convert_fusion
  71.9 2043.6 %while.23 = (s32[]{:T(128)}, f32[6,8,2,96]{3,2,1,0:T(2,128)S(1)}, f32[6,8,2,96]{3,2,1,0:T(2,128)S(1)}, f32[6,8,2,96,256]{4,3,2,1,0:T(8,128)}, bf16[6,96,8,256]{3...) while((s32[]{:T(128)}, f32[6,8,2,96]{3,2,1,0:T(2,128)S(1)}, ...), condition=%wide.region_5.6_spmd, body=%wide.region_2.5_spmd.sunk | while | flops 920438784 | bytes 133890480 | solution.py:87
  73.0 31.5 %collective-permute-done = bf16[6,96,8,256]{3,1,2,0:T(8,128)(2,1)} collective-permute-done((bf16[6,96,8,256]{3,1,2,0:T(8,128)(2,1)}, bf16[6,96,8,256]{3,1,2,0:T(8,128)(2,1)}, u32[]{:S(2)}, u32[]{:S(2)}) %collective-permute-start) | collective-permute-done | bytes 2359328 | tf_op jit(solution)/shard_map/while/body/eval_jaxpr/ppermute | solution.py:81
  114.7 15.2 collective-permute-done.1
  138.9 31.6 %collective-permute-done = bf16[6,96,8,256]{3,1,2,0:T(8,128)(2,1)} collective-permute-done((bf16[6,96,8,256]{3,1,2,0:T(8,128)(2,1)}, bf16[6,96,8,256]{3,1,2,0:T(8,128)(2,1)}, u32[]{:S(2)}, u32[]{:S(2)}) %collective-permute-start) | collective-permute-done | bytes 2359328 | tf_op jit(solution)/shard_map/while/body/eval_jaxpr/ppermute | solution.py:81
  204.8 31.6 %collective-permute-done = bf16[6,96,8,256]{3,1,2,0:T(8,128)(2,1)} collective-permute-done((bf16[6,96,8,256]{3,1,2,0:T(8,128)(2,1)}, bf16[6,96,8,256]{3,1,2,0:T(8,128)(2,1)}, u32[]{:S(2)}, u32[]{:S(2)}) %collective-permute-start) | collective-permute-done | bytes 2359328 | tf_op jit(solution)/shard_map/while/body/eval_jaxpr/ppermute | solution.py:81
  246.4 15.2 collective-permute-done.1
  270.6 31.6 %collective-permute-done = bf16[6,96,8,256]{3,1,2,0:T(8,128)(2,1)} collective-permute-done((bf16[6,96,8,256]{3,1,2,0:T(8,128)(2,1)}, bf16[6,96,8,256]{3,1,2,0:T(8,128)(2,1)}, u32[]{:S(2)}, u32[]{:S(2)}) %collective-permute-start) | collective-permute-done | bytes 2359328 | tf_op jit(solution)/shard_map/while/body/eval_jaxpr/ppermute | solution.py:81
  312.3 15.2 collective-permute-done.1
  336.5 31.6 %collective-permute-done = bf16[6,96,8,256]{3,1,2,0:T(8,128)(2,1)} collective-permute-done((bf16[6,96,8,256]{3,1,2,0:T(8,128)(2,1)}, bf16[6,96,8,256]{3,1,2,0:T(8,128)(2,1)}, u32[]{:S(2)}, u32[]{:S(2)}) %collective-permute-start) | collective-permute-done | bytes 2359328 | tf_op jit(solution)/shard_map/while/body/eval_jaxpr/ppermute | solution.py:81
  378.2 15.2 collective-permute-done.1
  402.4 31.6 %collective-permute-done = bf16[6,96,8,256]{3,1,2,0:T(8,128)(2,1)} collective-permute-done((bf16[6,96,8,256]{3,1,2,0:T(8,128)(2,1)}, bf16[6,96,8,256]{3,1,2,0:T(8,128)(2,1)}, u32[]{:S(2)}, u32[]{:S(2)}) %collective-permute-start) | collective-permute-done | bytes 2359328 | tf_op jit(solution)/shard_map/while/body/eval_jaxpr/ppermute | solution.py:81
  444.1 15.2 collective-permute-done.1
  468.3 31.6 %collective-permute-done = bf16[6,96,8,256]{3,1,2,0:T(8,128)(2,1)} collective-permute-done((bf16[6,96,8,256]{3,1,2,0:T(8,128)(2,1)}, bf16[6,96,8,256]{3,1,2,0:T(8,128)(2,1)}, u32[]{:S(2)}, u32[]{:S(2)}) %collective-permute-start) | collective-permute-done | bytes 2359328 | tf_op jit(solution)/shard_map/while/body/eval_jaxpr/ppermute | solution.py:81
  510.0 15.2 collective-permute-done.1
  534.2 31.6 %collective-permute-done = bf16[6,96,8,256]{3,1,2,0:T(8,128)(2,1)} collective-permute-done((bf16[6,96,8,256]{3,1,2,0:T(8,128)(2,1)}, bf16[6,96,8,256]{3,1,2,0:T(8,128)(2,1)}, u32[]{:S(2)}, u32[]{:S(2)}) %collective-permute-start) | collective-permute-done | bytes 2359328 | tf_op jit(solution)/shard_map/while/body/eval_jaxpr/ppermute | solution.py:81
  575.9 15.2 collective-permute-done.1
  600.1 31.6 %collective-permute-done = bf16[6,96,8,256]{3,1,2,0:T(8,128)(2,1)} collective-permute-done((bf16[6,96,8,256]{3,1,2,0:T(8,128)(2,1)}, bf16[6,96,8,256]{3,1,2,0:T(8,128)(2,1)}, u32[]{:S(2)}, u32[]{:S(2)}) %collective-permute-start) | collective-permute-done | bytes 2359328 | tf_op jit(solution)/shard_map/while/body/eval_jaxpr/ppermute | solution.py:81
  641.8 15.2 collective-permute-done.1
  666.0 31.6 %collective-permute-done = bf16[6,96,8,256]{3,1,2,0:T(8,128)(2,1)} collective-permute-done((bf16[6,96,8,256]{3,1,2,0:T(8,128)(2,1)}, bf16[6,96,8,256]{3,1,2,0:T(8,128)(2,1)}, u32[]{:S(2)}, u32[]{:S(2)}) %collective-permute-start) | collective-permute-done | bytes 2359328 | tf_op jit(solution)/shard_map/while/body/eval_jaxpr/ppermute | solution.py:81
  707.6 15.2 collective-permute-done.1
  731.9 31.6 %collective-permute-done = bf16[6,96,8,256]{3,1,2,0:T(8,128)(2,1)} collective-permute-done((bf16[6,96,8,256]{3,1,2,0:T(8,128)(2,1)}, bf16[6,96,8,256]{3,1,2,0:T(8,128)(2,1)}, u32[]{:S(2)}, u32[]{:S(2)}) %collective-permute-start) | collective-permute-done | bytes 2359328 | tf_op jit(solution)/shard_map/while/body/eval_jaxpr/ppermute | solution.py:81
  773.5 15.2 collective-permute-done.1
  797.7 31.6 %collective-permute-done = bf16[6,96,8,256]{3,1,2,0:T(8,128)(2,1)} collective-permute-done((bf16[6,96,8,256]{3,1,2,0:T(8,128)(2,1)}, bf16[6,96,8,256]{3,1,2,0:T(8,128)(2,1)}, u32[]{:S(2)}, u32[]{:S(2)}) %collective-permute-start) | collective-permute-done | bytes 2359328 | tf_op jit(solution)/shard_map/while/body/eval_jaxpr/ppermute | solution.py:81
  839.4 15.2 collective-permute-done.1
  863.6 31.6 %collective-permute-done = bf16[6,96,8,256]{3,1,2,0:T(8,128)(2,1)} collective-permute-done((bf16[6,96,8,256]{3,1,2,0:T(8,128)(2,1)}, bf16[6,96,8,256]{3,1,2,0:T(8,128)(2,1)}, u32[]{:S(2)}, u32[]{:S(2)}) %collective-permute-start) | collective-permute-done | bytes 2359328 | tf_op jit(solution)/shard_map/while/body/eval_jaxpr/ppermute | solution.py:81
  905.3 15.2 collective-permute-done.1
  929.5 31.6 %collective-permute-done = bf16[6,96,8,256]{3,1,2,0:T(8,128)(2,1)} collective-permute-done((bf16[6,96,8,256]{3,1,2,0:T(8,128)(2,1)}, bf16[6,96,8,256]{3,1,2,0:T(8,128)(2,1)}, u32[]{:S(2)}, u32[]{:S(2)}) %collective-permute-start) | collective-permute-done | bytes 2359328 | tf_op jit(solution)/shard_map/while/body/eval_jaxpr/ppermute | solution.py:81
  971.2 15.2 collective-permute-done.1
  995.4 31.6 %collective-permute-done = bf16[6,96,8,256]{3,1,2,0:T(8,128)(2,1)} collective-permute-done((bf16[6,96,8,256]{3,1,2,0:T(8,128)(2,1)}, bf16[6,96,8,256]{3,1,2,0:T(8,128)(2,1)}, u32[]{:S(2)}, u32[]{:S(2)}) %collective-permute-start) | collective-permute-done | bytes 2359328 | tf_op jit(solution)/shard_map/while/body/eval_jaxpr/ppermute | solution.py:81
  1037.1 15.2 collective-permute-done.1
  1061.3 31.6 %collective-permute-done = bf16[6,96,8,256]{3,1,2,0:T(8,128)(2,1)} collective-permute-done((bf16[6,96,8,256]{3,1,2,0:T(8,128)(2,1)}, bf16[6,96,8,256]{3,1,2,0:T(8,128)(2,1)}, u32[]{:S(2)}, u32[]{:S(2)}) %collective-permute-start) | collective-permute-done | bytes 2359328 | tf_op jit(solution)/shard_map/while/body/eval_jaxpr/ppermute | solution.py:81
  1103.0 15.2 collective-permute-done.1
  1127.2 31.6 %collective-permute-done = bf16[6,96,8,256]{3,1,2,0:T(8,128)(2,1)} collective-permute-done((bf16[6,96,8,256]{3,1,2,0:T(8,128)(2,1)}, bf16[6,96,8,256]{3,1,2,0:T(8,128)(2,1)}, u32[]{:S(2)}, u32[]{:S(2)}) %collective-permute-start) | collective-permute-done | bytes 2359328 | tf_op jit(solution)/shard_map/while/body/eval_jaxpr/ppermute | solution.py:81
  1168.8 15.2 collective-permute-done.1
  1193.1 31.6 %collective-permute-done = bf16[6,96,8,256]{3,1,2,0:T(8,128)(2,1)} collective-permute-done((bf16[6,96,8,256]{3,1,2,0:T(8,128)(2,1)}, bf16[6,96,8,256]{3,1,2,0:T(8,128)(2,1)}, u32[]{:S(2)}, u32[]{:S(2)}) %collective-permute-start) | collective-permute-done | bytes 2359328 | tf_op jit(solution)/shard_map/while/body/eval_jaxpr/ppermute | solution.py:81
  1234.7 15.2 collective-permute-done.1
  1258.9 31.6 %collective-permute-done = bf16[6,96,8,256]{3,1,2,0:T(8,128)(2,1)} collective-permute-done((bf16[6,96,8,256]{3,1,2,0:T(8,128)(2,1)}, bf16[6,96,8,256]{3,1,2,0:T(8,128)(2,1)}, u32[]{:S(2)}, u32[]{:S(2)}) %collective-permute-start) | collective-permute-done | bytes 2359328 | tf_op jit(solution)/shard_map/while/body/eval_jaxpr/ppermute | solution.py:81
  1300.6 15.2 collective-permute-done.1
  1324.8 31.6 %collective-permute-done = bf16[6,96,8,256]{3,1,2,0:T(8,128)(2,1)} collective-permute-done((bf16[6,96,8,256]{3,1,2,0:T(8,128)(2,1)}, bf16[6,96,8,256]{3,1,2,0:T(8,128)(2,1)}, u32[]{:S(2)}, u32[]{:S(2)}) %collective-permute-start) | collective-permute-done | bytes 2359328 | tf_op jit(solution)/shard_map/while/body/eval_jaxpr/ppermute | solution.py:81
  1366.5 15.2 collective-permute-done.1
  1390.7 31.6 %collective-permute-done = bf16[6,96,8,256]{3,1,2,0:T(8,128)(2,1)} collective-permute-done((bf16[6,96,8,256]{3,1,2,0:T(8,128)(2,1)}, bf16[6,96,8,256]{3,1,2,0:T(8,128)(2,1)}, u32[]{:S(2)}, u32[]{:S(2)}) %collective-permute-start) | collective-permute-done | bytes 2359328 | tf_op jit(solution)/shard_map/while/body/eval_jaxpr/ppermute | solution.py:81
  1432.4 15.2 collective-permute-done.1
  1456.6 31.6 %collective-permute-done = bf16[6,96,8,256]{3,1,2,0:T(8,128)(2,1)} collective-permute-done((bf16[6,96,8,256]{3,1,2,0:T(8,128)(2,1)}, bf16[6,96,8,256]{3,1,2,0:T(8,128)(2,1)}, u32[]{:S(2)}, u32[]{:S(2)}) %collective-permute-start) | collective-permute-done | bytes 2359328 | tf_op jit(solution)/shard_map/while/body/eval_jaxpr/ppermute | solution.py:81
  1498.3 15.2 collective-permute-done.1
  1522.5 31.6 %collective-permute-done = bf16[6,96,8,256]{3,1,2,0:T(8,128)(2,1)} collective-permute-done((bf16[6,96,8,256]{3,1,2,0:T(8,128)(2,1)}, bf16[6,96,8,256]{3,1,2,0:T(8,128)(2,1)}, u32[]{:S(2)}, u32[]{:S(2)}) %collective-permute-start) | collective-permute-done | bytes 2359328 | tf_op jit(solution)/shard_map/while/body/eval_jaxpr/ppermute | solution.py:81
  1564.2 15.2 collective-permute-done.1
  1588.4 31.6 %collective-permute-done = bf16[6,96,8,256]{3,1,2,0:T(8,128)(2,1)} collective-permute-done((bf16[6,96,8,256]{3,1,2,0:T(8,128)(2,1)}, bf16[6,96,8,256]{3,1,2,0:T(8,128)(2,1)}, u32[]{:S(2)}, u32[]{:S(2)}) %collective-permute-start) | collective-permute-done | bytes 2359328 | tf_op jit(solution)/shard_map/while/body/eval_jaxpr/ppermute | solution.py:81
  1630.1 15.2 collective-permute-done.1
  1654.3 31.6 %collective-permute-done = bf16[6,96,8,256]{3,1,2,0:T(8,128)(2,1)} collective-permute-done((bf16[6,96,8,256]{3,1,2,0:T(8,128)(2,1)}, bf16[6,96,8,256]{3,1,2,0:T(8,128)(2,1)}, u32[]{:S(2)}, u32[]{:S(2)}) %collective-permute-start) | collective-permute-done | bytes 2359328 | tf_op jit(solution)/shard_map/while/body/eval_jaxpr/ppermute | solution.py:81
  1695.9 15.2 collective-permute-done.1
  1720.1 31.6 %collective-permute-done = bf16[6,96,8,256]{3,1,2,0:T(8,128)(2,1)} collective-permute-done((bf16[6,96,8,256]{3,1,2,0:T(8,128)(2,1)}, bf16[6,96,8,256]{3,1,2,0:T(8,128)(2,1)}, u32[]{:S(2)}, u32[]{:S(2)}) %collective-permute-start) | collective-permute-done | bytes 2359328 | tf_op jit(solution)/shard_map/while/body/eval_jaxpr/ppermute | solution.py:81
  1761.8 15.2 collective-permute-done.1
  1786.0 31.6 %collective-permute-done = bf16[6,96,8,256]{3,1,2,0:T(8,128)(2,1)} collective-permute-done((bf16[6,96,8,256]{3,1,2,0:T(8,128)(2,1)}, bf16[6,96,8,256]{3,1,2,0:T(8,128)(2,1)}, u32[]{:S(2)}, u32[]{:S(2)}) %collective-permute-start) | collective-permute-done | bytes 2359328 | tf_op jit(solution)/shard_map/while/body/eval_jaxpr/ppermute | solution.py:81
  1827.7 15.2 collective-permute-done.1
  1851.9 31.6 %collective-permute-done = bf16[6,96,8,256]{3,1,2,0:T(8,128)(2,1)} collective-permute-done((bf16[6,96,8,256]{3,1,2,0:T(8,128)(2,1)}, bf16[6,96,8,256]{3,1,2,0:T(8,128)(2,1)}, u32[]{:S(2)}, u32[]{:S(2)}) %collective-permute-start) | collective-permute-done | bytes 2359328 | tf_op jit(solution)/shard_map/while/body/eval_jaxpr/ppermute | solution.py:81
  1893.6 15.2 collective-permute-done.1
  1917.8 31.6 %collective-permute-done = bf16[6,96,8,256]{3,1,2,0:T(8,128)(2,1)} collective-permute-done((bf16[6,96,8,256]{3,1,2,0:T(8,128)(2,1)}, bf16[6,96,8,256]{3,1,2,0:T(8,128)(2,1)}, u32[]{:S(2)}, u32[]{:S(2)}) %collective-permute-start) | collective-permute-done | bytes 2359328 | tf_op jit(solution)/shard_map/while/body/eval_jaxpr/ppermute | solution.py:81
  1959.5 15.2 collective-permute-done.1
  1983.7 31.6 %collective-permute-done = bf16[6,96,8,256]{3,1,2,0:T(8,128)(2,1)} collective-permute-done((bf16[6,96,8,256]{3,1,2,0:T(8,128)(2,1)}, bf16[6,96,8,256]{3,1,2,0:T(8,128)(2,1)}, u32[]{:S(2)}, u32[]{:S(2)}) %collective-permute-start) | collective-permute-done | bytes 2359328 | tf_op jit(solution)/shard_map/while/body/eval_jaxpr/ppermute | solution.py:81
  2025.4 15.2 collective-permute-done.1
  2049.6 31.6 %collective-permute-done = bf16[6,96,8,256]{3,1,2,0:T(8,128)(2,1)} collective-permute-done((bf16[6,96,8,256]{3,1,2,0:T(8,128)(2,1)}, bf16[6,96,8,256]{3,1,2,0:T(8,128)(2,1)}, u32[]{:S(2)}, u32[]{:S(2)}) %collective-permute-start) | collective-permute-done | bytes 2359328 | tf_op jit(solution)/shard_map/while/body/eval_jaxpr/ppermute | solution.py:81
  2091.3 15.2 collective-permute-done.1
  2115.5 27.2 %fusion.24 = bf16[6,96,3584]{2,1,0:T(8,128)(2,1)} fusion(bf16[6,96,3584]{2,1,0:T(8,128)(2,1)} %param.8, bf16[8,2,256,3584,1]{3,2,1,0,4:T(8,128)(2,1)} %bitcast.132, f32[6,8,2,96,256]{4,3,2,1,0:T(8,128)} %get-tuple-element.205, f32[6,8,2,96]{3,2,1,0:T(2,128)S(1)} %get-tuple-element.206), kind=kOutput, calls=%fused_computation.32 | convolution fusion | flops 16922345472 | bytes 47091712 | tf_op jit(solution)/shard_map/clhrf,lhfe->cre/dot_general | solution.py:63
  (615 shorter events, 658.0 us)
Async XLA Ops:
  71.9 32.7 %collective-permute-start = (bf16[6,96,8,256]{3,1,2,0:T(8,128)(2,1)}, bf16[6,96,8,256]{3,1,2,0:T(8,128)(2,1)}, u32[]{:S(2)}, u32[]{:S(2)}) collective-permute-start(bf16[6,96,8,256]{3,1,2,0:T(8,128)(2,1)} %get-tuple-element.314), channel_id=1, source_target_pairs={{0,1},{1,2},{2,3},{3,4},{4,5},{5,6},{6,7},{7,8},{8,9},{9,10},{10,1... | collective-permute-start | bytes 7077896 | tf_op jit(solution)/shard_map/while/body/eval_jaxpr/ppermute | solution.py:81
  71.9 58.0 %collective-permute-start.1 = (bf16[6,96,8,256]{3,1,2,0:T(8,128)(2,1)}, bf16[6,96,8,256]{3,1,2,0:T(8,128)(2,1)S(1)}, u32[]{:S(2)}, u32[]{:S(2)}) collective-permute-start(bf16[6,96,8,256]{3,1,2,0:T(8,128)(2,1)} %get-tuple-element.315), channel_id=1, source_target_pairs={{0,1},{1,2},{2,3},{3,4},{4,5},{5,6},{6,7},{7,8},{8,9},{9,10},{10,1... | collective-permute-start | bytes 7077896 | tf_op jit(solution)/shard_map/while/body/eval_jaxpr/ppermute | solution.py:82
  104.6 26.7 %slice-start.1 = ((s8[9437184]{0:T(1024)(128)(4,1)}), s8[4194304]{0:T(1024)(128)(4,1)S(1)}, s32[]{:S(2)}) async-start(s8[9437184]{0:T(1024)(128)(4,1)} %bitcast.122), calls=%async_computation.1 | async-start | bytes 8388608 | tf_op jit(solution)/shard_map/while
  138.9 31.6 %collective-permute-start = (bf16[6,96,8,256]{3,1,2,0:T(8,128)(2,1)}, bf16[6,96,8,256]{3,1,2,0:T(8,128)(2,1)}, u32[]{:S(2)}, u32[]{:S(2)}) collective-permute-start(bf16[6,96,8,256]{3,1,2,0:T(8,128)(2,1)} %get-tuple-element.314), channel_id=1, source_target_pairs={{0,1},{1,2},{2,3},{3,4},{4,5},{5,6},{6,7},{7,8},{8,9},{9,10},{10,1... | collective-permute-start | bytes 7077896 | tf_op jit(solution)/shard_map/while/body/eval_jaxpr/ppermute | solution.py:81
  138.9 56.9 %collective-permute-start.1 = (bf16[6,96,8,256]{3,1,2,0:T(8,128)(2,1)}, bf16[6,96,8,256]{3,1,2,0:T(8,128)(2,1)S(1)}, u32[]{:S(2)}, u32[]{:S(2)}) collective-permute-start(bf16[6,96,8,256]{3,1,2,0:T(8,128)(2,1)} %get-tuple-element.315), channel_id=1, source_target_pairs={{0,1},{1,2},{2,3},{3,4},{4,5},{5,6},{6,7},{7,8},{8,9},{9,10},{10,1... | collective-permute-start | bytes 7077896 | tf_op jit(solution)/shard_map/while/body/eval_jaxpr/ppermute | solution.py:82
  170.5 26.7 %slice-start.1 = ((s8[9437184]{0:T(1024)(128)(4,1)}), s8[4194304]{0:T(1024)(128)(4,1)S(1)}, s32[]{:S(2)}) async-start(s8[9437184]{0:T(1024)(128)(4,1)} %bitcast.122), calls=%async_computation.1 | async-start | bytes 8388608 | tf_op jit(solution)/shard_map/while
  204.8 31.6 %collective-permute-start = (bf16[6,96,8,256]{3,1,2,0:T(8,128)(2,1)}, bf16[6,96,8,256]{3,1,2,0:T(8,128)(2,1)}, u32[]{:S(2)}, u32[]{:S(2)}) collective-permute-start(bf16[6,96,8,256]{3,1,2,0:T(8,128)(2,1)} %get-tuple-element.314), channel_id=1, source_target_pairs={{0,1},{1,2},{2,3},{3,4},{4,5},{5,6},{6,7},{7,8},{8,9},{9,10},{10,1... | collective-permute-start | bytes 7077896 | tf_op jit(solution)/shard_map/while/body/eval_jaxpr/ppermute | solution.py:81
  204.8 56.9 %collective-permute-start.1 = (bf16[6,96,8,256]{3,1,2,0:T(8,128)(2,1)}, bf16[6,96,8,256]{3,1,2,0:T(8,128)(2,1)S(1)}, u32[]{:S(2)}, u32[]{:S(2)}) collective-permute-start(bf16[6,96,8,256]{3,1,2,0:T(8,128)(2,1)} %get-tuple-element.315), channel_id=1, source_target_pairs={{0,1},{1,2},{2,3},{3,4},{4,5},{5,6},{6,7},{7,8},{8,9},{9,10},{10,1... | collective-permute-start | bytes 7077896 | tf_op jit(solution)/shard_map/while/body/eval_jaxpr/ppermute | solution.py:82
  270.6 31.6 %collective-permute-start = (bf16[6,96,8,256]{3,1,2,0:T(8,128)(2,1)}, bf16[6,96,8,256]{3,1,2,0:T(8,128)(2,1)}, u32[]{:S(2)}, u32[]{:S(2)}) collective-permute-start(bf16[6,96,8,256]{3,1,2,0:T(8,128)(2,1)} %get-tuple-element.314), channel_id=1, source_target_pairs={{0,1},{1,2},{2,3},{3,4},{4,5},{5,6},{6,7},{7,8},{8,9},{9,10},{10,1... | collective-permute-start | bytes 7077896 | tf_op jit(solution)/shard_map/while/body/eval_jaxpr/ppermute | solution.py:81
  270.6 56.9 %collective-permute-start.1 = (bf16[6,96,8,256]{3,1,2,0:T(8,128)(2,1)}, bf16[6,96,8,256]{3,1,2,0:T(8,128)(2,1)S(1)}, u32[]{:S(2)}, u32[]{:S(2)}) collective-permute-start(bf16[6,96,8,256]{3,1,2,0:T(8,128)(2,1)} %get-tuple-element.315), channel_id=1, source_target_pairs={{0,1},{1,2},{2,3},{3,4},{4,5},{5,6},{6,7},{7,8},{8,9},{9,10},{10,1... | collective-permute-start | bytes 7077896 | tf_op jit(solution)/shard_map/while/body/eval_jaxpr/ppermute | solution.py:82
  336.5 31.6 %collective-permute-start = (bf16[6,96,8,256]{3,1,2,0:T(8,128)(2,1)}, bf16[6,96,8,256]{3,1,2,0:T(8,128)(2,1)}, u32[]{:S(2)}, u32[]{:S(2)}) collective-permute-start(bf16[6,96,8,256]{3,1,2,0:T(8,128)(2,1)} %get-tuple-element.314), channel_id=1, source_target_pairs={{0,1},{1,2},{2,3},{3,4},{4,5},{5,6},{6,7},{7,8},{8,9},{9,10},{10,1... | collective-permute-start | bytes 7077896 | tf_op jit(solution)/shard_map/while/body/eval_jaxpr/ppermute | solution.py:81
  336.5 56.9 %collective-permute-start.1 = (bf16[6,96,8,256]{3,1,2,0:T(8,128)(2,1)}, bf16[6,96,8,256]{3,1,2,0:T(8,128)(2,1)S(1)}, u32[]{:S(2)}, u32[]{:S(2)}) collective-permute-start(bf16[6,96,8,256]{3,1,2,0:T(8,128)(2,1)} %get-tuple-element.315), channel_id=1, source_target_pairs={{0,1},{1,2},{2,3},{3,4},{4,5},{5,6},{6,7},{7,8},{8,9},{9,10},{10,1... | collective-permute-start | bytes 7077896 | tf_op jit(solution)/shard_map/while/body/eval_jaxpr/ppermute | solution.py:82
  402.4 31.6 %collective-permute-start = (bf16[6,96,8,256]{3,1,2,0:T(8,128)(2,1)}, bf16[6,96,8,256]{3,1,2,0:T(8,128)(2,1)}, u32[]{:S(2)}, u32[]{:S(2)}) collective-permute-start(bf16[6,96,8,256]{3,1,2,0:T(8,128)(2,1)} %get-tuple-element.314), channel_id=1, source_target_pairs={{0,1},{1,2},{2,3},{3,4},{4,5},{5,6},{6,7},{7,8},{8,9},{9,10},{10,1... | collective-permute-start | bytes 7077896 | tf_op jit(solution)/shard_map/while/body/eval_jaxpr/ppermute | solution.py:81
  402.4 56.9 %collective-permute-start.1 = (bf16[6,96,8,256]{3,1,2,0:T(8,128)(2,1)}, bf16[6,96,8,256]{3,1,2,0:T(8,128)(2,1)S(1)}, u32[]{:S(2)}, u32[]{:S(2)}) collective-permute-start(bf16[6,96,8,256]{3,1,2,0:T(8,128)(2,1)} %get-tuple-element.315), channel_id=1, source_target_pairs={{0,1},{1,2},{2,3},{3,4},{4,5},{5,6},{6,7},{7,8},{8,9},{9,10},{10,1... | collective-permute-start | bytes 7077896 | tf_op jit(solution)/shard_map/while/body/eval_jaxpr/ppermute | solution.py:82
  468.3 31.6 %collective-permute-start = (bf16[6,96,8,256]{3,1,2,0:T(8,128)(2,1)}, bf16[6,96,8,256]{3,1,2,0:T(8,128)(2,1)}, u32[]{:S(2)}, u32[]{:S(2)}) collective-permute-start(bf16[6,96,8,256]{3,1,2,0:T(8,128)(2,1)} %get-tuple-element.314), channel_id=1, source_target_pairs={{0,1},{1,2},{2,3},{3,4},{4,5},{5,6},{6,7},{7,8},{8,9},{9,10},{10,1... | collective-permute-start | bytes 7077896 | tf_op jit(solution)/shard_map/while/body/eval_jaxpr/ppermute | solution.py:81
  468.3 56.9 %collective-permute-start.1 = (bf16[6,96,8,256]{3,1,2,0:T(8,128)(2,1)}, bf16[6,96,8,256]{3,1,2,0:T(8,128)(2,1)S(1)}, u32[]{:S(2)}, u32[]{:S(2)}) collective-permute-start(bf16[6,96,8,256]{3,1,2,0:T(8,128)(2,1)} %get-tuple-element.315), channel_id=1, source_target_pairs={{0,1},{1,2},{2,3},{3,4},{4,5},{5,6},{6,7},{7,8},{8,9},{9,10},{10,1... | collective-permute-start | bytes 7077896 | tf_op jit(solution)/shard_map/while/body/eval_jaxpr/ppermute | solution.py:82
  534.2 31.6 %collective-permute-start = (bf16[6,96,8,256]{3,1,2,0:T(8,128)(2,1)}, bf16[6,96,8,256]{3,1,2,0:T(8,128)(2,1)}, u32[]{:S(2)}, u32[]{:S(2)}) collective-permute-start(bf16[6,96,8,256]{3,1,2,0:T(8,128)(2,1)} %get-tuple-element.314), channel_id=1, source_target_pairs={{0,1},{1,2},{2,3},{3,4},{4,5},{5,6},{6,7},{7,8},{8,9},{9,10},{10,1... | collective-permute-start | bytes 7077896 | tf_op jit(solution)/shard_map/while/body/eval_jaxpr/ppermute | solution.py:81
  534.2 56.9 %collective-permute-start.1 = (bf16[6,96,8,256]{3,1,2,0:T(8,128)(2,1)}, bf16[6,96,8,256]{3,1,2,0:T(8,128)(2,1)S(1)}, u32[]{:S(2)}, u32[]{:S(2)}) collective-permute-start(bf16[6,96,8,256]{3,1,2,0:T(8,128)(2,1)} %get-tuple-element.315), channel_id=1, source_target_pairs={{0,1},{1,2},{2,3},{3,4},{4,5},{5,6},{6,7},{7,8},{8,9},{9,10},{10,1... | collective-permute-start | bytes 7077896 | tf_op jit(solution)/shard_map/while/body/eval_jaxpr/ppermute | solution.py:82
  600.1 31.6 %collective-permute-start = (bf16[6,96,8,256]{3,1,2,0:T(8,128)(2,1)}, bf16[6,96,8,256]{3,1,2,0:T(8,128)(2,1)}, u32[]{:S(2)}, u32[]{:S(2)}) collective-permute-start(bf16[6,96,8,256]{3,1,2,0:T(8,128)(2,1)} %get-tuple-element.314), channel_id=1, source_target_pairs={{0,1},{1,2},{2,3},{3,4},{4,5},{5,6},{6,7},{7,8},{8,9},{9,10},{10,1... | collective-permute-start | bytes 7077896 | tf_op jit(solution)/shard_map/while/body/eval_jaxpr/ppermute | solution.py:81
  600.1 56.9 %collective-permute-start.1 = (bf16[6,96,8,256]{3,1,2,0:T(8,128)(2,1)}, bf16[6,96,8,256]{3,1,2,0:T(8,128)(2,1)S(1)}, u32[]{:S(2)}, u32[]{:S(2)}) collective-permute-start(bf16[6,96,8,256]{3,1,2,0:T(8,128)(2,1)} %get-tuple-element.315), channel_id=1, source_target_pairs={{0,1},{1,2},{2,3},{3,4},{4,5},{5,6},{6,7},{7,8},{8,9},{9,10},{10,1... | collective-permute-start | bytes 7077896 | tf_op jit(solution)/shard_map/while/body/eval_jaxpr/ppermute | solution.py:82
  666.0 31.6 %collective-permute-start = (bf16[6,96,8,256]{3,1,2,0:T(8,128)(2,1)}, bf16[6,96,8,256]{3,1,2,0:T(8,128)(2,1)}, u32[]{:S(2)}, u32[]{:S(2)}) collective-permute-start(bf16[6,96,8,256]{3,1,2,0:T(8,128)(2,1)} %get-tuple-element.314), channel_id=1, source_target_pairs={{0,1},{1,2},{2,3},{3,4},{4,5},{5,6},{6,7},{7,8},{8,9},{9,10},{10,1... | collective-permute-start | bytes 7077896 | tf_op jit(solution)/shard_map/while/body/eval_jaxpr/ppermute | solution.py:81
  666.0 56.9 %collective-permute-start.1 = (bf16[6,96,8,256]{3,1,2,0:T(8,128)(2,1)}, bf16[6,96,8,256]{3,1,2,0:T(8,128)(2,1)S(1)}, u32[]{:S(2)}, u32[]{:S(2)}) collective-permute-start(bf16[6,96,8,256]{3,1,2,0:T(8,128)(2,1)} %get-tuple-element.315), channel_id=1, source_target_pairs={{0,1},{1,2},{2,3},{3,4},{4,5},{5,6},{6,7},{7,8},{8,9},{9,10},{10,1... | collective-permute-start | bytes 7077896 | tf_op jit(solution)/shard_map/while/body/eval_jaxpr/ppermute | solution.py:82
  731.8 31.6 %collective-permute-start = (bf16[6,96,8,256]{3,1,2,0:T(8,128)(2,1)}, bf16[6,96,8,256]{3,1,2,0:T(8,128)(2,1)}, u32[]{:S(2)}, u32[]{:S(2)}) collective-permute-start(bf16[6,96,8,256]{3,1,2,0:T(8,128)(2,1)} %get-tuple-element.314), channel_id=1, source_target_pairs={{0,1},{1,2},{2,3},{3,4},{4,5},{5,6},{6,7},{7,8},{8,9},{9,10},{10,1... | collective-permute-start | bytes 7077896 | tf_op jit(solution)/shard_map/while/body/eval_jaxpr/ppermute | solution.py:81
  731.9 56.9 %collective-permute-start.1 = (bf16[6,96,8,256]{3,1,2,0:T(8,128)(2,1)}, bf16[6,96,8,256]{3,1,2,0:T(8,128)(2,1)S(1)}, u32[]{:S(2)}, u32[]{:S(2)}) collective-permute-start(bf16[6,96,8,256]{3,1,2,0:T(8,128)(2,1)} %get-tuple-element.315), channel_id=1, source_target_pairs={{0,1},{1,2},{2,3},{3,4},{4,5},{5,6},{6,7},{7,8},{8,9},{9,10},{10,1... | collective-permute-start | bytes 7077896 | tf_op jit(solution)/shard_map/while/body/eval_jaxpr/ppermute | solution.py:82
  797.7 31.6 %collective-permute-start = (bf16[6,96,8,256]{3,1,2,0:T(8,128)(2,1)}, bf16[6,96,8,256]{3,1,2,0:T(8,128)(2,1)}, u32[]{:S(2)}, u32[]{:S(2)}) collective-permute-start(bf16[6,96,8,256]{3,1,2,0:T(8,128)(2,1)} %get-tuple-element.314), channel_id=1, source_target_pairs={{0,1},{1,2},{2,3},{3,4},{4,5},{5,6},{6,7},{7,8},{8,9},{9,10},{10,1... | collective-permute-start | bytes 7077896 | tf_op jit(solution)/shard_map/while/body/eval_jaxpr/ppermute | solution.py:81
  797.7 56.9 %collective-permute-start.1 = (bf16[6,96,8,256]{3,1,2,0:T(8,128)(2,1)}, bf16[6,96,8,256]{3,1,2,0:T(8,128)(2,1)S(1)}, u32[]{:S(2)}, u32[]{:S(2)}) collective-permute-start(bf16[6,96,8,256]{3,1,2,0:T(8,128)(2,1)} %get-tuple-element.315), channel_id=1, source_target_pairs={{0,1},{1,2},{2,3},{3,4},{4,5},{5,6},{6,7},{7,8},{8,9},{9,10},{10,1... | collective-permute-start | bytes 7077896 | tf_op jit(solution)/shard_map/while/body/eval_jaxpr/ppermute | solution.py:82
  863.6 31.6 %collective-permute-start = (bf16[6,96,8,256]{3,1,2,0:T(8,128)(2,1)}, bf16[6,96,8,256]{3,1,2,0:T(8,128)(2,1)}, u32[]{:S(2)}, u32[]{:S(2)}) collective-permute-start(bf16[6,96,8,256]{3,1,2,0:T(8,128)(2,1)} %get-tuple-element.314), channel_id=1, source_target_pairs={{0,1},{1,2},{2,3},{3,4},{4,5},{5,6},{6,7},{7,8},{8,9},{9,10},{10,1... | collective-permute-start | bytes 7077896 | tf_op jit(solution)/shard_map/while/body/eval_jaxpr/ppermute | solution.py:81
  863.6 56.9 %collective-permute-start.1 = (bf16[6,96,8,256]{3,1,2,0:T(8,128)(2,1)}, bf16[6,96,8,256]{3,1,2,0:T(8,128)(2,1)S(1)}, u32[]{:S(2)}, u32[]{:S(2)}) collective-permute-start(bf16[6,96,8,256]{3,1,2,0:T(8,128)(2,1)} %get-tuple-element.315), channel_id=1, source_target_pairs={{0,1},{1,2},{2,3},{3,4},{4,5},{5,6},{6,7},{7,8},{8,9},{9,10},{10,1... | collective-permute-start | bytes 7077896 | tf_op jit(solution)/shard_map/while/body/eval_jaxpr/ppermute | solution.py:82
  929.5 31.6 %collective-permute-start = (bf16[6,96,8,256]{3,1,2,0:T(8,128)(2,1)}, bf16[6,96,8,256]{3,1,2,0:T(8,128)(2,1)}, u32[]{:S(2)}, u32[]{:S(2)}) collective-permute-start(bf16[6,96,8,256]{3,1,2,0:T(8,128)(2,1)} %get-tuple-element.314), channel_id=1, source_target_pairs={{0,1},{1,2},{2,3},{3,4},{4,5},{5,6},{6,7},{7,8},{8,9},{9,10},{10,1... | collective-permute-start | bytes 7077896 | tf_op jit(solution)/shard_map/while/body/eval_jaxpr/ppermute | solution.py:81
  929.5 56.9 %collective-permute-start.1 = (bf16[6,96,8,256]{3,1,2,0:T(8,128)(2,1)}, bf16[6,96,8,256]{3,1,2,0:T(8,128)(2,1)S(1)}, u32[]{:S(2)}, u32[]{:S(2)}) collective-permute-start(bf16[6,96,8,256]{3,1,2,0:T(8,128)(2,1)} %get-tuple-element.315), channel_id=1, source_target_pairs={{0,1},{1,2},{2,3},{3,4},{4,5},{5,6},{6,7},{7,8},{8,9},{9,10},{10,1... | collective-permute-start | bytes 7077896 | tf_op jit(solution)/shard_map/while/body/eval_jaxpr/ppermute | solution.py:82
  995.4 31.6 %collective-permute-start = (bf16[6,96,8,256]{3,1,2,0:T(8,128)(2,1)}, bf16[6,96,8,256]{3,1,2,0:T(8,128)(2,1)}, u32[]{:S(2)}, u32[]{:S(2)}) collective-permute-start(bf16[6,96,8,256]{3,1,2,0:T(8,128)(2,1)} %get-tuple-element.314), channel_id=1, source_target_pairs={{0,1},{1,2},{2,3},{3,4},{4,5},{5,6},{6,7},{7,8},{8,9},{9,10},{10,1... | collective-permute-start | bytes 7077896 | tf_op jit(solution)/shard_map/while/body/eval_jaxpr/ppermute | solution.py:81
  995.4 56.9 %collective-permute-start.1 = (bf16[6,96,8,256]{3,1,2,0:T(8,128)(2,1)}, bf16[6,96,8,256]{3,1,2,0:T(8,128)(2,1)S(1)}, u32[]{:S(2)}, u32[]{:S(2)}) collective-permute-start(bf16[6,96,8,256]{3,1,2,0:T(8,128)(2,1)} %get-tuple-element.315), channel_id=1, source_target_pairs={{0,1},{1,2},{2,3},{3,4},{4,5},{5,6},{6,7},{7,8},{8,9},{9,10},{10,1... | collective-permute-start | bytes 7077896 | tf_op jit(solution)/shard_map/while/body/eval_jaxpr/ppermute | solution.py:82
  1061.3 31.6 %collective-permute-start = (bf16[6,96,8,256]{3,1,2,0:T(8,128)(2,1)}, bf16[6,96,8,256]{3,1,2,0:T(8,128)(2,1)}, u32[]{:S(2)}, u32[]{:S(2)}) collective-permute-start(bf16[6,96,8,256]{3,1,2,0:T(8,128)(2,1)} %get-tuple-element.314), channel_id=1, source_target_pairs={{0,1},{1,2},{2,3},{3,4},{4,5},{5,6},{6,7},{7,8},{8,9},{9,10},{10,1... | collective-permute-start | bytes 7077896 | tf_op jit(solution)/shard_map/while/body/eval_jaxpr/ppermute | solution.py:81
  1061.3 56.9 %collective-permute-start.1 = (bf16[6,96,8,256]{3,1,2,0:T(8,128)(2,1)}, bf16[6,96,8,256]{3,1,2,0:T(8,128)(2,1)S(1)}, u32[]{:S(2)}, u32[]{:S(2)}) collective-permute-start(bf16[6,96,8,256]{3,1,2,0:T(8,128)(2,1)} %get-tuple-element.315), channel_id=1, source_target_pairs={{0,1},{1,2},{2,3},{3,4},{4,5},{5,6},{6,7},{7,8},{8,9},{9,10},{10,1... | collective-permute-start | bytes 7077896 | tf_op jit(solution)/shard_map/while/body/eval_jaxpr/ppermute | solution.py:82
  1127.2 31.6 %collective-permute-start = (bf16[6,96,8,256]{3,1,2,0:T(8,128)(2,1)}, bf16[6,96,8,256]{3,1,2,0:T(8,128)(2,1)}, u32[]{:S(2)}, u32[]{:S(2)}) collective-permute-start(bf16[6,96,8,256]{3,1,2,0:T(8,128)(2,1)} %get-tuple-element.314), channel_id=1, source_target_pairs={{0,1},{1,2},{2,3},{3,4},{4,5},{5,6},{6,7},{7,8},{8,9},{9,10},{10,1... | collective-permute-start | bytes 7077896 | tf_op jit(solution)/shard_map/while/body/eval_jaxpr/ppermute | solution.py:81
  1127.2 56.9 %collective-permute-start.1 = (bf16[6,96,8,256]{3,1,2,0:T(8,128)(2,1)}, bf16[6,96,8,256]{3,1,2,0:T(8,128)(2,1)S(1)}, u32[]{:S(2)}, u32[]{:S(2)}) collective-permute-start(bf16[6,96,8,256]{3,1,2,0:T(8,128)(2,1)} %get-tuple-element.315), channel_id=1, source_target_pairs={{0,1},{1,2},{2,3},{3,4},{4,5},{5,6},{6,7},{7,8},{8,9},{9,10},{10,1... | collective-permute-start | bytes 7077896 | tf_op jit(solution)/shard_map/while/body/eval_jaxpr/ppermute | solution.py:82
  1193.1 31.6 %collective-permute-start = (bf16[6,96,8,256]{3,1,2,0:T(8,128)(2,1)}, bf16[6,96,8,256]{3,1,2,0:T(8,128)(2,1)}, u32[]{:S(2)}, u32[]{:S(2)}) collective-permute-start(bf16[6,96,8,256]{3,1,2,0:T(8,128)(2,1)} %get-tuple-element.314), channel_id=1, source_target_pairs={{0,1},{1,2},{2,3},{3,4},{4,5},{5,6},{6,7},{7,8},{8,9},{9,10},{10,1... | collective-permute-start | bytes 7077896 | tf_op jit(solution)/shard_map/while/body/eval_jaxpr/ppermute | solution.py:81
  1193.1 56.9 %collective-permute-start.1 = (bf16[6,96,8,256]{3,1,2,0:T(8,128)(2,1)}, bf16[6,96,8,256]{3,1,2,0:T(8,128)(2,1)S(1)}, u32[]{:S(2)}, u32[]{:S(2)}) collective-permute-start(bf16[6,96,8,256]{3,1,2,0:T(8,128)(2,1)} %get-tuple-element.315), channel_id=1, source_target_pairs={{0,1},{1,2},{2,3},{3,4},{4,5},{5,6},{6,7},{7,8},{8,9},{9,10},{10,1... | collective-permute-start | bytes 7077896 | tf_op jit(solution)/shard_map/while/body/eval_jaxpr/ppermute | solution.py:82
  1258.9 31.6 %collective-permute-start = (bf16[6,96,8,256]{3,1,2,0:T(8,128)(2,1)}, bf16[6,96,8,256]{3,1,2,0:T(8,128)(2,1)}, u32[]{:S(2)}, u32[]{:S(2)}) collective-permute-start(bf16[6,96,8,256]{3,1,2,0:T(8,128)(2,1)} %get-tuple-element.314), channel_id=1, source_target_pairs={{0,1},{1,2},{2,3},{3,4},{4,5},{5,6},{6,7},{7,8},{8,9},{9,10},{10,1... | collective-permute-start | bytes 7077896 | tf_op jit(solution)/shard_map/while/body/eval_jaxpr/ppermute | solution.py:81
  1258.9 56.9 %collective-permute-start.1 = (bf16[6,96,8,256]{3,1,2,0:T(8,128)(2,1)}, bf16[6,96,8,256]{3,1,2,0:T(8,128)(2,1)S(1)}, u32[]{:S(2)}, u32[]{:S(2)}) collective-permute-start(bf16[6,96,8,256]{3,1,2,0:T(8,128)(2,1)} %get-tuple-element.315), channel_id=1, source_target_pairs={{0,1},{1,2},{2,3},{3,4},{4,5},{5,6},{6,7},{7,8},{8,9},{9,10},{10,1... | collective-permute-start | bytes 7077896 | tf_op jit(solution)/shard_map/while/body/eval_jaxpr/ppermute | solution.py:82
  1324.8 31.6 %collective-permute-start = (bf16[6,96,8,256]{3,1,2,0:T(8,128)(2,1)}, bf16[6,96,8,256]{3,1,2,0:T(8,128)(2,1)}, u32[]{:S(2)}, u32[]{:S(2)}) collective-permute-start(bf16[6,96,8,256]{3,1,2,0:T(8,128)(2,1)} %get-tuple-element.314), channel_id=1, source_target_pairs={{0,1},{1,2},{2,3},{3,4},{4,5},{5,6},{6,7},{7,8},{8,9},{9,10},{10,1... | collective-permute-start | bytes 7077896 | tf_op jit(solution)/shard_map/while/body/eval_jaxpr/ppermute | solution.py:81
  1324.8 56.9 %collective-permute-start.1 = (bf16[6,96,8,256]{3,1,2,0:T(8,128)(2,1)}, bf16[6,96,8,256]{3,1,2,0:T(8,128)(2,1)S(1)}, u32[]{:S(2)}, u32[]{:S(2)}) collective-permute-start(bf16[6,96,8,256]{3,1,2,0:T(8,128)(2,1)} %get-tuple-element.315), channel_id=1, source_target_pairs={{0,1},{1,2},{2,3},{3,4},{4,5},{5,6},{6,7},{7,8},{8,9},{9,10},{10,1... | collective-permute-start | bytes 7077896 | tf_op jit(solution)/shard_map/while/body/eval_jaxpr/ppermute | solution.py:82
  1390.7 31.6 %collective-permute-start = (bf16[6,96,8,256]{3,1,2,0:T(8,128)(2,1)}, bf16[6,96,8,256]{3,1,2,0:T(8,128)(2,1)}, u32[]{:S(2)}, u32[]{:S(2)}) collective-permute-start(bf16[6,96,8,256]{3,1,2,0:T(8,128)(2,1)} %get-tuple-element.314), channel_id=1, source_target_pairs={{0,1},{1,2},{2,3},{3,4},{4,5},{5,6},{6,7},{7,8},{8,9},{9,10},{10,1... | collective-permute-start | bytes 7077896 | tf_op jit(solution)/shard_map/while/body/eval_jaxpr/ppermute | solution.py:81
  1390.7 56.9 %collective-permute-start.1 = (bf16[6,96,8,256]{3,1,2,0:T(8,128)(2,1)}, bf16[6,96,8,256]{3,1,2,0:T(8,128)(2,1)S(1)}, u32[]{:S(2)}, u32[]{:S(2)}) collective-permute-start(bf16[6,96,8,256]{3,1,2,0:T(8,128)(2,1)} %get-tuple-element.315), channel_id=1, source_target_pairs={{0,1},{1,2},{2,3},{3,4},{4,5},{5,6},{6,7},{7,8},{8,9},{9,10},{10,1... | collective-permute-start | bytes 7077896 | tf_op jit(solution)/shard_map/while/body/eval_jaxpr/ppermute | solution.py:82
  1456.6 31.6 %collective-permute-start = (bf16[6,96,8,256]{3,1,2,0:T(8,128)(2,1)}, bf16[6,96,8,256]{3,1,2,0:T(8,128)(2,1)}, u32[]{:S(2)}, u32[]{:S(2)}) collective-permute-start(bf16[6,96,8,256]{3,1,2,0:T(8,128)(2,1)} %get-tuple-element.314), channel_id=1, source_target_pairs={{0,1},{1,2},{2,3},{3,4},{4,5},{5,6},{6,7},{7,8},{8,9},{9,10},{10,1... | collective-permute-start | bytes 7077896 | tf_op jit(solution)/shard_map/while/body/eval_jaxpr/ppermute | solution.py:81
  1456.6 56.9 %collective-permute-start.1 = (bf16[6,96,8,256]{3,1,2,0:T(8,128)(2,1)}, bf16[6,96,8,256]{3,1,2,0:T(8,128)(2,1)S(1)}, u32[]{:S(2)}, u32[]{:S(2)}) collective-permute-start(bf16[6,96,8,256]{3,1,2,0:T(8,128)(2,1)} %get-tuple-element.315), channel_id=1, source_target_pairs={{0,1},{1,2},{2,3},{3,4},{4,5},{5,6},{6,7},{7,8},{8,9},{9,10},{10,1... | collective-permute-start | bytes 7077896 | tf_op jit(solution)/shard_map/while/body/eval_jaxpr/ppermute | solution.py:82
  1522.5 31.6 %collective-permute-start = (bf16[6,96,8,256]{3,1,2,0:T(8,128)(2,1)}, bf16[6,96,8,256]{3,1,2,0:T(8,128)(2,1)}, u32[]{:S(2)}, u32[]{:S(2)}) collective-permute-start(bf16[6,96,8,256]{3,1,2,0:T(8,128)(2,1)} %get-tuple-element.314), channel_id=1, source_target_pairs={{0,1},{1,2},{2,3},{3,4},{4,5},{5,6},{6,7},{7,8},{8,9},{9,10},{10,1... | collective-permute-start | bytes 7077896 | tf_op jit(solution)/shard_map/while/body/eval_jaxpr/ppermute | solution.py:81
  1522.5 56.9 %collective-permute-start.1 = (bf16[6,96,8,256]{3,1,2,0:T(8,128)(2,1)}, bf16[6,96,8,256]{3,1,2,0:T(8,128)(2,1)S(1)}, u32[]{:S(2)}, u32[]{:S(2)}) collective-permute-start(bf16[6,96,8,256]{3,1,2,0:T(8,128)(2,1)} %get-tuple-element.315), channel_id=1, source_target_pairs={{0,1},{1,2},{2,3},{3,4},{4,5},{5,6},{6,7},{7,8},{8,9},{9,10},{10,1... | collective-permute-start | bytes 7077896 | tf_op jit(solution)/shard_map/while/body/eval_jaxpr/ppermute | solution.py:82
  1588.4 31.6 %collective-permute-start = (bf16[6,96,8,256]{3,1,2,0:T(8,128)(2,1)}, bf16[6,96,8,256]{3,1,2,0:T(8,128)(2,1)}, u32[]{:S(2)}, u32[]{:S(2)}) collective-permute-start(bf16[6,96,8,256]{3,1,2,0:T(8,128)(2,1)} %get-tuple-element.314), channel_id=1, source_target_pairs={{0,1},{1,2},{2,3},{3,4},{4,5},{5,6},{6,7},{7,8},{8,9},{9,10},{10,1... | collective-permute-start | bytes 7077896 | tf_op jit(solution)/shard_map/while/body/eval_jaxpr/ppermute | solution.py:81
  1588.4 56.9 %collective-permute-start.1 = (bf16[6,96,8,256]{3,1,2,0:T(8,128)(2,1)}, bf16[6,96,8,256]{3,1,2,0:T(8,128)(2,1)S(1)}, u32[]{:S(2)}, u32[]{:S(2)}) collective-permute-start(bf16[6,96,8,256]{3,1,2,0:T(8,128)(2,1)} %get-tuple-element.315), channel_id=1, source_target_pairs={{0,1},{1,2},{2,3},{3,4},{4,5},{5,6},{6,7},{7,8},{8,9},{9,10},{10,1... | collective-permute-start | bytes 7077896 | tf_op jit(solution)/shard_map/while/body/eval_jaxpr/ppermute | solution.py:82
  1654.3 31.6 %collective-permute-start = (bf16[6,96,8,256]{3,1,2,0:T(8,128)(2,1)}, bf16[6,96,8,256]{3,1,2,0:T(8,128)(2,1)}, u32[]{:S(2)}, u32[]{:S(2)}) collective-permute-start(bf16[6,96,8,256]{3,1,2,0:T(8,128)(2,1)} %get-tuple-element.314), channel_id=1, source_target_pairs={{0,1},{1,2},{2,3},{3,4},{4,5},{5,6},{6,7},{7,8},{8,9},{9,10},{10,1... | collective-permute-start | bytes 7077896 | tf_op jit(solution)/shard_map/while/body/eval_jaxpr/ppermute | solution.py:81
  1654.3 56.9 %collective-permute-start.1 = (bf16[6,96,8,256]{3,1,2,0:T(8,128)(2,1)}, bf16[6,96,8,256]{3,1,2,0:T(8,128)(2,1)S(1)}, u32[]{:S(2)}, u32[]{:S(2)}) collective-permute-start(bf16[6,96,8,256]{3,1,2,0:T(8,128)(2,1)} %get-tuple-element.315), channel_id=1, source_target_pairs={{0,1},{1,2},{2,3},{3,4},{4,5},{5,6},{6,7},{7,8},{8,9},{9,10},{10,1... | collective-permute-start | bytes 7077896 | tf_op jit(solution)/shard_map/while/body/eval_jaxpr/ppermute | solution.py:82
  1720.1 31.6 %collective-permute-start = (bf16[6,96,8,256]{3,1,2,0:T(8,128)(2,1)}, bf16[6,96,8,256]{3,1,2,0:T(8,128)(2,1)}, u32[]{:S(2)}, u32[]{:S(2)}) collective-permute-start(bf16[6,96,8,256]{3,1,2,0:T(8,128)(2,1)} %get-tuple-element.314), channel_id=1, source_target_pairs={{0,1},{1,2},{2,3},{3,4},{4,5},{5,6},{6,7},{7,8},{8,9},{9,10},{10,1... | collective-permute-start | bytes 7077896 | tf_op jit(solution)/shard_map/while/body/eval_jaxpr/ppermute | solution.py:81
  1720.1 56.9 %collective-permute-start.1 = (bf16[6,96,8,256]{3,1,2,0:T(8,128)(2,1)}, bf16[6,96,8,256]{3,1,2,0:T(8,128)(2,1)S(1)}, u32[]{:S(2)}, u32[]{:S(2)}) collective-permute-start(bf16[6,96,8,256]{3,1,2,0:T(8,128)(2,1)} %get-tuple-element.315), channel_id=1, source_target_pairs={{0,1},{1,2},{2,3},{3,4},{4,5},{5,6},{6,7},{7,8},{8,9},{9,10},{10,1... | collective-permute-start | bytes 7077896 | tf_op jit(solution)/shard_map/while/body/eval_jaxpr/ppermute | solution.py:82
  1786.0 31.6 %collective-permute-start = (bf16[6,96,8,256]{3,1,2,0:T(8,128)(2,1)}, bf16[6,96,8,256]{3,1,2,0:T(8,128)(2,1)}, u32[]{:S(2)}, u32[]{:S(2)}) collective-permute-start(bf16[6,96,8,256]{3,1,2,0:T(8,128)(2,1)} %get-tuple-element.314), channel_id=1, source_target_pairs={{0,1},{1,2},{2,3},{3,4},{4,5},{5,6},{6,7},{7,8},{8,9},{9,10},{10,1... | collective-permute-start | bytes 7077896 | tf_op jit(solution)/shard_map/while/body/eval_jaxpr/ppermute | solution.py:81
  1786.0 56.9 %collective-permute-start.1 = (bf16[6,96,8,256]{3,1,2,0:T(8,128)(2,1)}, bf16[6,96,8,256]{3,1,2,0:T(8,128)(2,1)S(1)}, u32[]{:S(2)}, u32[]{:S(2)}) collective-permute-start(bf16[6,96,8,256]{3,1,2,0:T(8,128)(2,1)} %get-tuple-element.315), channel_id=1, source_target_pairs={{0,1},{1,2},{2,3},{3,4},{4,5},{5,6},{6,7},{7,8},{8,9},{9,10},{10,1... | collective-permute-start | bytes 7077896 | tf_op jit(solution)/shard_map/while/body/eval_jaxpr/ppermute | solution.py:82
  1851.9 31.6 %collective-permute-start = (bf16[6,96,8,256]{3,1,2,0:T(8,128)(2,1)}, bf16[6,96,8,256]{3,1,2,0:T(8,128)(2,1)}, u32[]{:S(2)}, u32[]{:S(2)}) collective-permute-start(bf16[6,96,8,256]{3,1,2,0:T(8,128)(2,1)} %get-tuple-element.314), channel_id=1, source_target_pairs={{0,1},{1,2},{2,3},{3,4},{4,5},{5,6},{6,7},{7,8},{8,9},{9,10},{10,1... | collective-permute-start | bytes 7077896 | tf_op jit(solution)/shard_map/while/body/eval_jaxpr/ppermute | solution.py:81
  1851.9 56.9 %collective-permute-start.1 = (bf16[6,96,8,256]{3,1,2,0:T(8,128)(2,1)}, bf16[6,96,8,256]{3,1,2,0:T(8,128)(2,1)S(1)}, u32[]{:S(2)}, u32[]{:S(2)}) collective-permute-start(bf16[6,96,8,256]{3,1,2,0:T(8,128)(2,1)} %get-tuple-element.315), channel_id=1, source_target_pairs={{0,1},{1,2},{2,3},{3,4},{4,5},{5,6},{6,7},{7,8},{8,9},{9,10},{10,1... | collective-permute-start | bytes 7077896 | tf_op jit(solution)/shard_map/while/body/eval_jaxpr/ppermute | solution.py:82
  1917.8 31.6 %collective-permute-start = (bf16[6,96,8,256]{3,1,2,0:T(8,128)(2,1)}, bf16[6,96,8,256]{3,1,2,0:T(8,128)(2,1)}, u32[]{:S(2)}, u32[]{:S(2)}) collective-permute-start(bf16[6,96,8,256]{3,1,2,0:T(8,128)(2,1)} %get-tuple-element.314), channel_id=1, source_target_pairs={{0,1},{1,2},{2,3},{3,4},{4,5},{5,6},{6,7},{7,8},{8,9},{9,10},{10,1... | collective-permute-start | bytes 7077896 | tf_op jit(solution)/shard_map/while/body/eval_jaxpr/ppermute | solution.py:81
  1917.8 56.9 %collective-permute-start.1 = (bf16[6,96,8,256]{3,1,2,0:T(8,128)(2,1)}, bf16[6,96,8,256]{3,1,2,0:T(8,128)(2,1)S(1)}, u32[]{:S(2)}, u32[]{:S(2)}) collective-permute-start(bf16[6,96,8,256]{3,1,2,0:T(8,128)(2,1)} %get-tuple-element.315), channel_id=1, source_target_pairs={{0,1},{1,2},{2,3},{3,4},{4,5},{5,6},{6,7},{7,8},{8,9},{9,10},{10,1... | collective-permute-start | bytes 7077896 | tf_op jit(solution)/shard_map/while/body/eval_jaxpr/ppermute | solution.py:82
  1983.7 31.6 %collective-permute-start = (bf16[6,96,8,256]{3,1,2,0:T(8,128)(2,1)}, bf16[6,96,8,256]{3,1,2,0:T(8,128)(2,1)}, u32[]{:S(2)}, u32[]{:S(2)}) collective-permute-start(bf16[6,96,8,256]{3,1,2,0:T(8,128)(2,1)} %get-tuple-element.314), channel_id=1, source_target_pairs={{0,1},{1,2},{2,3},{3,4},{4,5},{5,6},{6,7},{7,8},{8,9},{9,10},{10,1... | collective-permute-start | bytes 7077896 | tf_op jit(solution)/shard_map/while/body/eval_jaxpr/ppermute | solution.py:81
  1983.7 56.9 %collective-permute-start.1 = (bf16[6,96,8,256]{3,1,2,0:T(8,128)(2,1)}, bf16[6,96,8,256]{3,1,2,0:T(8,128)(2,1)S(1)}, u32[]{:S(2)}, u32[]{:S(2)}) collective-permute-start(bf16[6,96,8,256]{3,1,2,0:T(8,128)(2,1)} %get-tuple-element.315), channel_id=1, source_target_pairs={{0,1},{1,2},{2,3},{3,4},{4,5},{5,6},{6,7},{7,8},{8,9},{9,10},{10,1... | collective-permute-start | bytes 7077896 | tf_op jit(solution)/shard_map/while/body/eval_jaxpr/ppermute | solution.py:82
  2049.6 31.6 %collective-permute-start = (bf16[6,96,8,256]{3,1,2,0:T(8,128)(2,1)}, bf16[6,96,8,256]{3,1,2,0:T(8,128)(2,1)}, u32[]{:S(2)}, u32[]{:S(2)}) collective-permute-start(bf16[6,96,8,256]{3,1,2,0:T(8,128)(2,1)} %get-tuple-element.314), channel_id=1, source_target_pairs={{0,1},{1,2},{2,3},{3,4},{4,5},{5,6},{6,7},{7,8},{8,9},{9,10},{10,1... | collective-permute-start | bytes 7077896 | tf_op jit(solution)/shard_map/while/body/eval_jaxpr/ppermute | solution.py:81
  2049.6 56.9 %collective-permute-start.1 = (bf16[6,96,8,256]{3,1,2,0:T(8,128)(2,1)}, bf16[6,96,8,256]{3,1,2,0:T(8,128)(2,1)S(1)}, u32[]{:S(2)}, u32[]{:S(2)}) collective-permute-start(bf16[6,96,8,256]{3,1,2,0:T(8,128)(2,1)} %get-tuple-element.315), channel_id=1, source_target_pairs={{0,1},{1,2},{2,3},{3,4},{4,5},{5,6},{6,7},{7,8},{8,9},{9,10},{10,1... | collective-permute-start | bytes 7077896 | tf_op jit(solution)/shard_map/while/body/eval_jaxpr/ppermute | solution.py:82
  (127 other events, 2352.6 us)
where the time goes:
time: 2140 us
  waiting for transfers between devices  1450 us (68%)
  matrix products  364 us (17%)
  local copies, waits for them, and re-layouts  264 us (12%)
  other arithmetic  61.7 us (3%)
    ppermute x31, waiting for transfers between devices, kv_step(): k_cur = lax.ppermute(k_cur, 'cp', shift_pairs)  979 us
    ppermute x31, waiting for transfers between devices, kv_step(): v_cur = lax.ppermute(v_cur, 'cp', shift_pairs)  471 us
    while x341, local copies, waits for them, and re-layouts  263 us
    dot_general x32, matrix products, block_update(): jnp.einsum('bqkge,bske->bkgqs', queries, k_blk, preferred_element_type=jn...  164 us
    dot_general x32, matrix products, block_update(): jnp.einsum('bkgqs,bske->bkgqe', p_weights.astype(jnp.bfloat16), v_blk, pr...  127 us
    reduce_sum x32, other arithmetic, block_update(): run_sum = run_sum * correction + jnp.sum(p_weights, axis=-1)  47.3 us
  transfers between devices with their start and end apart: 62, of which 62 were waited for; matrix products, arithmetic and copies ran while one was open for 15% of the time, Pallas kernels for 0%

commit v1 on v0

v1 whole, which is shorter than its diff:
```python
import functools

import jax
import jax.numpy as jnp
from jax import lax
from jax.experimental import pallas as pl
from jax.experimental.pallas import tpu as pltpu
from jax.sharding import PartitionSpec as P

ROPE_BASE = 500000.0
LOG2E = 1.4426950408889634


def rope_tables(positions, head_dim):
    inv_freq = ROPE_BASE ** (-jnp.arange(0, head_dim, 2, dtype=jnp.float32) / head_dim)
    angles = positions.astype(jnp.float32)[..., None] * inv_freq
    angles = jnp.concatenate([angles, angles], axis=-1)
    return jnp.cos(angles)[:, :, None, :], jnp.sin(angles)[:, :, None, :]


def rope_apply(in_vals, cos_tab, sin_tab):
    half_dim = in_vals.shape[-1] // 2
    val_f32 = in_vals.astype(jnp.float32)
    rotated = jnp.concatenate([-val_f32[..., half_dim:], val_f32[..., :half_dim]], axis=-1)
    return (val_f32 * cos_tab + rotated * sin_tab).astype(jnp.bfloat16)


def project(hidden, weights):
    return jnp.einsum('bsd,dhe->bshe', hidden, weights, preferred_element_type=jnp.float32).astype(jnp.bfloat16)


def flash_kernel(blk, q_ref, mine_ref, o_ref, kv_ref, copy_sem, send_sem, recv_sem):
    seq, head_dim = q_ref.shape
    me = lax.axis_index('cp')
    core = lax.rem(me, 2)
    partner = {'cp': me + 1 - 2 * core}
    barrier = pltpu.get_barrier_semaphore()
    pl.semaphore_signal(barrier, inc=1, device_id=partner, device_id_type=pl.DeviceIdType.MESH)
    keep = pltpu.make_async_copy(mine_ref, kv_ref.at[core], copy_sem)
    keep.start()
    pl.semaphore_wait(barrier, 1)
    share = pltpu.make_async_remote_copy(
        src_ref=mine_ref,
        dst_ref=kv_ref.at[core],
        send_sem=send_sem,
        recv_sem=recv_sem,
        device_id=partner,
        device_id_type=pl.DeviceIdType.MESH,
    )
    share.start()
    keep.wait()
    share.wait()
    scale = (head_dim ** -0.5) * LOG2E
    for c in range(seq // blk):
        rows, width = pl.ds(c * blk, blk), (c + 1) * blk
        scores = lax.dot_general(
            q_ref[rows, :], kv_ref[0, pl.ds(0, width), :], (((1,), (1,)), ((), ())), preferred_element_type=jnp.float32
        )
        row_ids = lax.broadcasted_iota(jnp.int32, (blk, width), 0) + c * blk
        col_ids = lax.broadcasted_iota(jnp.int32, (blk, width), 1)
        scores = jnp.where(col_ids <= row_ids, scores, -jnp.inf)
        row_max = jnp.max(scores, axis=1, keepdims=True)
        p_weights = jnp.exp2((scores - row_max) * scale)
        row_sum = jnp.sum(p_weights, axis=1, keepdims=True)
        out = jnp.dot(p_weights.astype(jnp.bfloat16), kv_ref[1, pl.ds(0, width), :], preferred_element_type=jnp.float32)
        o_ref[rows, :] = (out / row_sum).astype(o_ref.dtype)


def flash(queries, mine, collective_id):
    seq, head_dim = queries.shape
    blk = 256 if seq % 256 == 0 else 96
    return pl.pallas_call(
        functools.partial(flash_kernel, blk),
        out_shape=jax.ShapeDtypeStruct((seq, head_dim), jnp.bfloat16),
        in_specs=[pl.BlockSpec(memory_space=pltpu.VMEM), pl.BlockSpec(memory_space=pl.ANY)],
        out_specs=pl.BlockSpec(memory_space=pltpu.VMEM),
        scratch_shapes=[
            pltpu.VMEM((2, seq, head_dim), jnp.bfloat16),
            pltpu.SemaphoreType.DMA,
            pltpu.SemaphoreType.DMA,
            pltpu.SemaphoreType.DMA,
        ],
        compiler_params=pltpu.CompilerParams(collective_id=collective_id, has_side_effects=True),
        cost_estimate=pl.CostEstimate(flops=2 * seq * seq * head_dim, bytes_accessed=8 * seq * head_dim, transcendentals=seq * seq // 2),
        name='flash',
    )(queries, mine)


def solution(mesh):
    cp_size = mesh.shape['cp']

    def per_device(hidden, positions, w_q, w_k, w_v, w_o):
        n_seq, tok_dev, width = hidden.shape
        n_heads, head_dim = w_q.shape[1], w_q.shape[2]
        n_kv = w_k.shape[1]
        per_round = cp_size // n_heads
        n_rounds = n_seq // per_round
        seq_len = cp_size * tok_dev
        cos_tab, sin_tab = rope_tables(positions, head_dim)

        def exchange(blocks):
            return lax.all_to_all(blocks.reshape(cp_size, tok_dev, head_dim), 'cp', 0, 0)

        k_rot = rope_apply(project(hidden, w_k), cos_tab, sin_tab).transpose(0, 2, 1, 3)
        values = project(hidden, w_v).transpose(0, 2, 1, 3)
        kv_send = jnp.stack([k_rot, values], axis=2)
        queries = rope_apply(project(hidden, w_q), cos_tab, sin_tab).transpose(0, 2, 1, 3)
        outs = []
        for r in range(n_rounds):
            part = slice(r * per_round, (r + 1) * per_round)
            kv_mine = exchange(kv_send[part])
            q_mine = exchange(queries[part])
            o_mine = flash(q_mine.reshape(seq_len, head_dim), kv_mine.reshape(seq_len, head_dim), r + 1)
            outs.append(exchange(o_mine).reshape(per_round, n_heads, tok_dev, head_dim))
        o_back = jnp.concatenate(outs, axis=0)
        proj_out = jnp.einsum('bhse,hed->bsd', o_back, w_o, preferred_element_type=jnp.float32)
        return (hidden.astype(jnp.float32) + proj_out).astype(jnp.bfloat16)

    rep_spec = P(None, None, None)
    return jax.shard_map(per_device, mesh=mesh, in_specs=(P('dp', 'cp', None), P('dp', 'cp'), rep_spec, rep_spec, rep_spec, rep_spec), out_specs=P('dp', 'cp', None), check_vma=False)
```

time: 2140 us -> 321 us (0.15)
  the two profiles are of different devices: /device:TPU:96 before, /device:TPU:97 now
where the time goes in v1:
time: 321 us; the launch traced here: 315 us
  blocking collectives  82.7 us (26%)
  matrix products  72.6 us (23%)
  waiting for transfers between devices  69.8 us (22%)
  Pallas kernels  44.5 us (14%)
  starting transfers between devices  28.8 us (9%)
  local copies, waits for them, and re-layouts  7.81 us (2%)
  other arithmetic  7.67 us (2%)
    all_to_all x3, blocking collectives, exchange(): lax.all_to_all(blocks.reshape(cp_size, tok_dev, head_dim), 'cp', 0, 0)  82.7 us
    all_to_all x6, waiting for transfers between devices, exchange(): lax.all_to_all(blocks.reshape(cp_size, tok_dev, head_dim), 'cp', 0, 0)  69.8 us
    dot_general x3, matrix products, project(): jnp.einsum('bsd,dhe->bshe', hidden, weights, preferred_element_type=jnp.f...  47.8 us
    pallas_call x3, Pallas kernels, flash(): pl.pallas_call(functools.partial(flash_kernel, blk), out_shape=jax.ShapeD...  44.5 us
    all_to_all x6, starting transfers between devices, exchange(): lax.all_to_all(blocks.reshape(cp_size, tok_dev, head_dim), 'cp', 0, 0)  28.8 us
    dot_general x1, matrix products, per_device(): jnp.einsum('bhse,hed->bsd', o_back, w_o, preferred_element_type=jnp.float32)  24.9 us
  transfers between devices with their start and end apart: 6, of which 5 were waited for; matrix products, arithmetic and copies ran while one was open for 10% of the time, Pallas kernels for 14%

profile of v1, /device:TPU:97, one launch (start us, length us, event | category | flops | bytes accessed | tf_op | source)
XLA Modules:
  0.0 314.6 jit_solution(15427215015834343584)
XLA Ops:
  0.0 22.3 %convert_convert_fusion = f32[6,96,16,256]{3,1,2,0:T(8,128)S(1)} fusion(bf16[3584,16,256]{2,1,0:T(8,128)(2,1)} %param.8, bf16[6,96,3584]{2,1,0:T(8,128)(2,1)} %param.6), kind=kOutput, calls=%fused_computation.30 | convolution fusion | flops 16916152320 | bytes 42926080 | tf_op jit(solution)/shard_map/bsd,dhe->bshe/dot_general | solution.py:29
  22.3 0.0 copy-start.7
  22.3 1.3 slice_negate_fusion
  23.6 0.0 copy-done.7
  23.7 0.1 broadcast_multiply_fusion
  23.8 2.1 fusion.43
  25.9 0.0 copy-start.1
  25.9 0.0 copy-start.3
  25.9 0.8 copy-done.1
  26.7 0.2 copy-done.3
  26.9 1.9 fusion.16
  28.8 2.3 fusion.45
  31.1 10.1 %all-to-all-start.6 = ((bf16[32,96,256]{2,1,0:T(8,128)(2,1)}), bf16[32,96,256]{2,1,0:T(8,128)(2,1)}, u32[]{:S(2)}, u32[]{:S(2)}) async-start(bf16[32,96,256]{2,1,0:T(8,128)(2,1)} %bitcast.23), calls=%async_computation.6 | async-start | bytes 3145728 | tf_op jit(solution)/shard_map/all_to_all | solution.py:102
  41.2 0.0 copy-start
  41.2 13.4 %convert_convert_fusion.1 = f32[6,96,8,256]{3,1,2,0:T(8,128)S(1)} fusion(bf16[3584,8,256]{2,1,0:T(8,128)(2,1)} %param.9, bf16[6,96,3584]{2,1,0:T(8,128)(2,1)} %param.6), kind=kOutput, calls=%fused_computation.37 | convolution fusion | flops 8458076160 | bytes 23527424 | tf_op jit(solution)/shard_map/bsd,dhe->bshe/dot_general | solution.py:29
  54.6 0.0 copy-done
  54.6 12.1 %convert_bitcast_fusion = bf16[6,8,1,96,256]{4,3,1,0,2:T(8,128)(2,1)S(1)} fusion(bf16[3584,8,256]{2,1,0:T(8,128)(2,1)} %param.10, bf16[6,96,3584]{2,1,0:T(8,128)(2,1)S(1)} %copy-done), kind=kOutput, calls=%fused_computation.36 | convolution fusion | flops 8456896512 | bytes 21168128 | tf_op jit(solution)/shard_map/bsd,dhe->bshe/dot_general | solution.py:29
  66.7 0.0 copy-start.2
  66.7 0.0 copy-start.4
  66.7 0.6 slice_negate_fusion.1
  67.4 0.4 copy-done.2
  67.8 0.2 copy-done.4
  68.0 1.1 fusion.31
  69.1 0.5 fusion.41
  69.6 1.3 copy.15
  70.9 0.0 all-to-all-done.6
  70.9 29.3 %all_to_all.45 = bf16[32,96,256]{2,1,0:T(8,128)(2,1)} all-to-all(bf16[32,96,256]{2,1,0:T(8,128)(2,1)} %bitcast.68), channel_id=1, replica_groups=mesh['dp'=1,'cp'=32] {'cp'}, dimensions={0} | all-to-all | bytes 3145728 | tf_op jit(solution)/shard_map/all_to_all | solution.py:102
  100.1 3.9 %all-to-all-start.3 = ((bf16[32,96,256]{2,1,0:T(8,128)(2,1)}), bf16[32,96,256]{2,1,0:T(8,128)(2,1)}, u32[]{:S(2)}, u32[]{:S(2)}) async-start(bf16[32,96,256]{2,1,0:T(8,128)(2,1)} %bitcast.17), calls=%async_computation.3 | async-start | bytes 3145728 | tf_op jit(solution)/shard_map/all_to_all | solution.py:102
  104.0 1.3 copy.14
  105.3 23.0 %all-to-all-done.3 = bf16[32,96,256]{2,1,0:T(8,128)(2,1)} async-done(((bf16[32,96,256]{2,1,0:T(8,128)(2,1)}), bf16[32,96,256]{2,1,0:T(8,128)(2,1)}, u32[]{:S(2)}, u32[]{:S(2)}) %all-to-all-start.3) | async-done | bytes 1572896 | tf_op jit(solution)/shard_map/all_to_all | solution.py:102
  128.3 26.8 %all_to_all.46 = bf16[32,96,256]{2,1,0:T(8,128)(2,1)} all-to-all(bf16[32,96,256]{2,1,0:T(8,128)(2,1)} %bitcast.69), channel_id=1, replica_groups=mesh['dp'=1,'cp'=32] {'cp'}, dimensions={0} | all-to-all | bytes 3145728 | tf_op jit(solution)/shard_map/all_to_all | solution.py:102
  155.2 3.1 all-to-all-start
  158.3 1.4 copy.13
  159.7 21.5 %all-to-all-done = bf16[32,96,256]{2,1,0:T(8,128)(2,1)S(1)} async-done(((bf16[32,96,256]{2,1,0:T(8,128)(2,1)}), bf16[32,96,256]{2,1,0:T(8,128)(2,1)S(1)}, u32[]{:S(2)}, u32[]{:S(2)}) %all-to-all-start) | async-done | bytes 1572896 | tf_op jit(solution)/shard_map/all_to_all | solution.py:102
  181.2 0.0 copy-start.5
  181.2 5.3 %all-to-all-start.1 = ((bf16[32,96,256]{2,1,0:T(8,128)(2,1)}), bf16[32,96,256]{2,1,0:T(8,128)(2,1)S(1)}, u32[]{:S(2)}, u32[]{:S(2)}) async-start(bf16[32,96,256]{2,1,0:T(8,128)(2,1)} %bitcast.13), calls=%async_computation.1 | async-start | bytes 3145728 | tf_op jit(solution)/shard_map/all_to_all | solution.py:102
  186.4 14.8 %flash.5 = bf16[3072,256]{1,0:T(8,128)(2,1)} custom-call(bf16[3072,256]{1,0:T(8,128)(2,1)} %bitcast.24.q_ref, bf16[3072,256]{1,0:T(8,128)(2,1)} %bitcast.71), custom_call_target="tpu_custom_call" | custom-call | flops 4831838208 | bytes 6291456 | tf_op jit(solution)/shard_map/flash/pallas_call | solution.py:72
  201.3 0.0 copy-done.5
  201.3 8.4 %all-to-all-done.1 = bf16[32,96,256]{2,1,0:T(8,128)(2,1)S(1)} async-done(((bf16[32,96,256]{2,1,0:T(8,128)(2,1)}), bf16[32,96,256]{2,1,0:T(8,128)(2,1)S(1)}, u32[]{:S(2)}, u32[]{:S(2)}) %all-to-all-start.1) | async-done | bytes 1572896 | tf_op jit(solution)/shard_map/all_to_all | solution.py:102
  209.7 0.0 copy-start.6
  209.7 3.2 %all-to-all-start.8 = ((bf16[32,96,256]{2,1,0:T(8,128)(2,1)}), bf16[32,96,256]{2,1,0:T(8,128)(2,1)S(1)}, u32[]{:S(2)}, u32[]{:S(2)}) async-start(bf16[32,96,256]{2,1,0:T(8,128)(2,1)} %bitcast.76), calls=%async_computation.8 | async-start | bytes 3145728 | tf_op jit(solution)/shard_map/all_to_all | solution.py:102
  212.9 14.8 %flash.4 = bf16[3072,256]{1,0:T(8,128)(2,1)} custom-call(bf16[3072,256]{1,0:T(8,128)(2,1)} %bitcast.18.q_ref, bf16[3072,256]{1,0:T(8,128)(2,1)} %bitcast.72), custom_call_target="tpu_custom_call" | custom-call | flops 4831838208 | bytes 6291456 | tf_op jit(solution)/shard_map/flash/pallas_call | solution.py:72
  227.8 0.0 copy-done.6
  227.8 8.4 %all-to-all-done.8 = bf16[32,96,256]{2,1,0:T(8,128)(2,1)S(1)} async-done(((bf16[32,96,256]{2,1,0:T(8,128)(2,1)}), bf16[32,96,256]{2,1,0:T(8,128)(2,1)S(1)}, u32[]{:S(2)}, u32[]{:S(2)}) %all-to-all-start.8) | async-done | bytes 1572896 | tf_op jit(solution)/shard_map/all_to_all | solution.py:102
  236.2 3.2 %all-to-all-start.5 = ((bf16[32,96,256]{2,1,0:T(8,128)(2,1)}), bf16[32,96,256]{2,1,0:T(8,128)(2,1)S(1)}, u32[]{:S(2)}, u32[]{:S(2)}) async-start(bf16[32,96,256]{2,1,0:T(8,128)(2,1)} %bitcast.77), calls=%async_computation.5 | async-start | bytes 3145728 | tf_op jit(solution)/shard_map/all_to_all | solution.py:102
  239.4 14.8 %flash.3 = bf16[3072,256]{1,0:T(8,128)(2,1)} custom-call(bf16[3072,256]{1,0:T(8,128)(2,1)} %bitcast.70, bf16[3072,256]{1,0:T(8,128)(2,1)} %bitcast.73), custom_call_target="tpu_custom_call" | custom-call | flops 4831838208 | bytes 6291456 | tf_op jit(solution)/shard_map/flash/pallas_call | solution.py:72
  254.3 8.4 %all-to-all-done.5 = bf16[32,96,256]{2,1,0:T(8,128)(2,1)S(1)} async-done(((bf16[32,96,256]{2,1,0:T(8,128)(2,1)}), bf16[32,96,256]{2,1,0:T(8,128)(2,1)S(1)}, u32[]{:S(2)}, u32[]{:S(2)}) %all-to-all-start.5) | async-done | bytes 1572896 | tf_op jit(solution)/shard_map/all_to_all | solution.py:102
  262.7 26.5 %all_to_all.47 = bf16[32,96,256]{2,1,0:T(8,128)(2,1)} all-to-all(bf16[32,96,256]{2,1,0:T(8,128)(2,1)} %bitcast.78), channel_id=1, replica_groups=mesh['dp'=1,'cp'=32] {'cp'}, dimensions={0} | all-to-all | bytes 3145728 | tf_op jit(solution)/shard_map/all_to_all | solution.py:102
  289.2 24.9 %fusion.13 = bf16[6,96,3584]{2,1,0:T(8,128)(2,1)} fusion(bf16[6,96,3584]{2,1,0:T(8,128)(2,1)} %param.6, bf16[16,256,3584]{2,1,0:T(8,128)(2,1)} %param.11, bf16[2,16,96,256]{3,2,1,0:T(8,128)(2,1)S(1)} %bitcast.74, bf16[2,16,96,256]{3,2,1,0:T(8,128)(2,1)S(1)} %bitcast.75, bf16[2,16,96,256]{3,2,1,0:T(8,128)(2,1)} %bitcast.79), kind=kOutput, calls=%fused_computation.15 | convolution fusion | flops 16922345472 | bytes 42336256 | tf_op jit(solution)/shard_map/bhse,hed->bsd/dot_general | solution.py:116
  (2 shorter events, 0.0 us)
Async XLA Ops:
  22.3 1.3 copy-start.7
  25.9 0.8 copy-start.1
  25.9 1.0 copy-start.3
  31.1 39.8 %all-to-all-start.6 = ((bf16[32,96,256]{2,1,0:T(8,128)(2,1)}), bf16[32,96,256]{2,1,0:T(8,128)(2,1)}, u32[]{:S(2)}, u32[]{:S(2)}) async-start(bf16[32,96,256]{2,1,0:T(8,128)(2,1)} %bitcast.23), calls=%async_computation.6 | async-start | bytes 3145728 | tf_op jit(solution)/shard_map/all_to_all | solution.py:102
  41.2 13.4 %copy-start = (bf16[6,96,3584]{2,1,0:T(8,128)(2,1)S(1)}, bf16[6,96,3584]{2,1,0:T(8,128)(2,1)}, u32[]{:S(2)}) copy-start(bf16[6,96,3584]{2,1,0:T(8,128)(2,1)} %param.6) | copy-start | bytes 12386308
  66.7 1.1 copy-start.2
  66.7 1.2 copy-start.4
  100.1 28.2 %all-to-all-start.3 = ((bf16[32,96,256]{2,1,0:T(8,128)(2,1)}), bf16[32,96,256]{2,1,0:T(8,128)(2,1)}, u32[]{:S(2)}, u32[]{:S(2)}) async-start(bf16[32,96,256]{2,1,0:T(8,128)(2,1)} %bitcast.17), calls=%async_computation.3 | async-start | bytes 3145728 | tf_op jit(solution)/shard_map/all_to_all | solution.py:102
  155.2 26.0 %all-to-all-start = ((bf16[32,96,256]{2,1,0:T(8,128)(2,1)}), bf16[32,96,256]{2,1,0:T(8,128)(2,1)S(1)}, u32[]{:S(2)}, u32[]{:S(2)}) async-start(bf16[32,96,256]{2,1,0:T(8,128)(2,1)} %bitcast.4), calls=%async_computation | async-start | bytes 3145728 | tf_op jit(solution)/shard_map/all_to_all | solution.py:102
  181.2 20.1 %copy-start.5 = (bf16[32,96,256]{2,1,0:T(8,128)(2,1)}, bf16[32,96,256]{2,1,0:T(8,128)(2,1)S(1)}, u32[]{:S(2)}) copy-start(bf16[32,96,256]{2,1,0:T(8,128)(2,1)S(1)} %all-to-all-done) | copy-start | bytes 4718596
  181.2 28.6 %all-to-all-start.1 = ((bf16[32,96,256]{2,1,0:T(8,128)(2,1)}), bf16[32,96,256]{2,1,0:T(8,128)(2,1)S(1)}, u32[]{:S(2)}, u32[]{:S(2)}) async-start(bf16[32,96,256]{2,1,0:T(8,128)(2,1)} %bitcast.13), calls=%async_computation.1 | async-start | bytes 3145728 | tf_op jit(solution)/shard_map/all_to_all | solution.py:102
  209.7 18.0 %copy-start.6 = (bf16[32,96,256]{2,1,0:T(8,128)(2,1)}, bf16[32,96,256]{2,1,0:T(8,128)(2,1)S(1)}, u32[]{:S(2)}) copy-start(bf16[32,96,256]{2,1,0:T(8,128)(2,1)S(1)} %all-to-all-done.1) | copy-start | bytes 4718596
  209.7 26.5 %all-to-all-start.8 = ((bf16[32,96,256]{2,1,0:T(8,128)(2,1)}), bf16[32,96,256]{2,1,0:T(8,128)(2,1)S(1)}, u32[]{:S(2)}, u32[]{:S(2)}) async-start(bf16[32,96,256]{2,1,0:T(8,128)(2,1)} %bitcast.76), calls=%async_computation.8 | async-start | bytes 3145728 | tf_op jit(solution)/shard_map/all_to_all | solution.py:102
  236.2 26.5 %all-to-all-start.5 = ((bf16[32,96,256]{2,1,0:T(8,128)(2,1)}), bf16[32,96,256]{2,1,0:T(8,128)(2,1)S(1)}, u32[]{:S(2)}, u32[]{:S(2)}) async-start(bf16[32,96,256]{2,1,0:T(8,128)(2,1)} %bitcast.77), calls=%async_computation.5 | async-start | bytes 3145728 | tf_op jit(solution)/shard_map/all_to_all | solution.py:102

commit v2 on v1

v2 whole, which is shorter than its diff:
```python
import functools
import math

import jax
import jax.numpy as jnp
from jax import lax
from jax.experimental import pallas as pl
from jax.experimental.pallas import tpu as pltpu
from jax.sharding import PartitionSpec as P

ROPE_BASE = 500000.0
LOG2E = 1.4426950408889634


def rope_tables(positions, head_dim):
    inv_freq = ROPE_BASE ** (-jnp.arange(0, head_dim, 2, dtype=jnp.float32) / head_dim)
    angles = positions.astype(jnp.float32)[..., None] * inv_freq
    angles = jnp.concatenate([angles, angles], axis=-1)
    return jnp.cos(angles)[:, :, None, :], jnp.sin(angles)[:, :, None, :]


def rope_apply(in_vals, cos_tab, sin_tab):
    half_dim = in_vals.shape[-1] // 2
    val_f32 = in_vals.astype(jnp.float32)
    rotated = jnp.concatenate([-val_f32[..., half_dim:], val_f32[..., :half_dim]], axis=-1)
    return (val_f32 * cos_tab + rotated * sin_tab).astype(jnp.bfloat16)


def project(hidden, weights):
    return jnp.einsum('bsd,dhe->bshe', hidden, weights, preferred_element_type=jnp.float32).astype(jnp.bfloat16)


def peer_offsets(side):
    order = []
    for dy in range(side):
        for dx in range(side):
            for dc in range(2):
                for a, b in ((dy, dx), (-dy % side, -dx % side), (dx, dy), (-dx % side, -dy % side)):
                    if (a, b, dc) != (0, 0, 0) and (a, b, dc) not in order:
                        order.append((a, b, dc))
    return order


def attend_kernel(
    blk, n_heads, q_hbm, kv_hbm, x_hbm, w_hbm, y_hbm, q_buf, kv_buf, o_buf, x_buf, w_buf,
    w_sem, x_sem, y_sem, q_own, q_send, q_recv, kv_own, kv_send, kv_recv, o_own, o_send, o_recv,
):
    n_rounds, n_dev, tok, head_dim = q_buf.shape
    side = math.isqrt(n_dev // 2)
    me = lax.axis_index('cp')
    core = lax.rem(me, 2)
    col = lax.rem(me // 2, side)
    row = me // (2 * side)
    partner = {'cp': me + 1 - 2 * core}
    peers = [
        (lax.rem(row + dy, side) * side + lax.rem(col + dx, side)) * 2 + lax.rem(core + dc, 2)
        for dy, dx, dc in peer_offsets(side)
    ]

    def remote(src, dst, send, recv, device):
        return pltpu.make_async_remote_copy(
            src_ref=src, dst_ref=dst, send_sem=send, recv_sem=recv, device_id=device,
            device_id_type=pl.DeviceIdType.MESH,
        )

    def all_peers(r, send, recv):
        blocks = q_buf.at[r, pl.ds(0, n_dev - 1)]
        return remote(blocks, blocks, send, recv, partner)

    barrier = pltpu.get_barrier_semaphore()
    for peer in peers:
        pl.semaphore_signal(barrier, inc=1, device_id={'cp': peer}, device_id_type=pl.DeviceIdType.MESH)
    hidden = pltpu.make_async_copy(x_hbm, x_buf, x_sem)

    def keep_kv(r):
        return pltpu.make_async_copy(kv_hbm.at[:, r], kv_buf.at[r, core], kv_own.at[r])

    def share_kv(r):
        return remote(kv_hbm.at[:, r], kv_buf.at[r, core], kv_send.at[r], kv_recv.at[r], partner)

    def keep_q(r):
        return pltpu.make_async_copy(q_hbm.at[r, me], q_buf.at[r, me], q_own.at[r])

    my_rows = pl.ds(pl.multiple_of((me // n_heads) * tok, tok), tok)
    my_lanes = pl.ds(pl.multiple_of(lax.rem(me, n_heads) * head_dim, head_dim), head_dim)

    def keep_o(r):
        return pltpu.make_async_copy(q_buf.at[r, me], o_buf.at[r, my_rows, my_lanes], o_own.at[r])

    for r in range(n_rounds):
        keep_kv(r).start()
        keep_q(r).start()
    pl.semaphore_wait(barrier, n_dev - 1)
    for r in range(n_rounds):
        share_kv(r).start()
        for peer in peers:
            remote(q_hbm.at[r, peer], q_buf.at[r, me], q_send.at[r], q_recv.at[r], {'cp': peer}).start()
    hidden.start()
    n_slots, _, tile = w_buf.shape
    n_tiles = x_buf.shape[2] // tile

    def load_w(g):
        slot = lax.rem(g, n_slots)
        cols = pl.ds(pl.multiple_of(lax.rem(g, n_tiles) * tile, tile), tile)
        return pltpu.make_async_copy(w_hbm.at[:, cols], w_buf.at[slot], w_sem.at[slot])

    for g in range(n_slots):
        load_w(g).start()
    scale = (head_dim ** -0.5) * LOG2E
    group = blk // tok

    def attend(r):
        for c in range(n_dev // group):
            width = (c + 1) * blk
            mine = pl.ds(c * group, group)
            before = pl.ds(0, (c + 1) * group)
            q_blk = q_buf[r, mine].reshape(blk, head_dim)
            keys = kv_buf[r, 0, before].reshape(width, head_dim)
            vals = kv_buf[r, 1, before].reshape(width, head_dim)
            scores = lax.dot_general(q_blk, keys, (((1,), (1,)), ((), ())), preferred_element_type=jnp.float32)
            row_ids = lax.broadcasted_iota(jnp.int32, (blk, width), 0) + c * blk
            col_ids = lax.broadcasted_iota(jnp.int32, (blk, width), 1)
            scores = jnp.where(col_ids <= row_ids, scores, -jnp.inf)
            row_max = jnp.max(scores, axis=1, keepdims=True)
            p_weights = jnp.exp2((scores - row_max) * scale)
            row_sum = jnp.sum(p_weights, axis=1, keepdims=True)
            out = jnp.dot(p_weights.astype(jnp.bfloat16), vals, preferred_element_type=jnp.float32)
            q_buf[r, mine] = (out / row_sum).astype(q_buf.dtype).reshape(group, tok, head_dim)

    def project_out(r):
        all_peers(r, o_send.at[r], o_recv.at[r]).wait_recv()
        keep_o(r).wait()

        @pl.loop(0, n_tiles)
        def _(t):
            g = r * n_tiles + t
            cols = pl.ds(pl.multiple_of(t * tile, tile), tile)
            load_w(g).wait()
            proj = jnp.dot(o_buf[r], w_buf[lax.rem(g, n_slots)], preferred_element_type=jnp.float32)
            x_buf[r, :, cols] = (x_buf[r, :, cols].astype(jnp.float32) + proj).astype(x_buf.dtype)

            @pl.when(g + n_slots < n_rounds * n_tiles)
            def _():
                load_w(g + n_slots).start()

        pltpu.make_async_copy(x_buf.at[r], y_hbm.at[r], y_sem.at[r]).start()

    @pl.loop(0, n_rounds)
    def _(r):
        keep_kv(r).wait()
        share_kv(r).wait_recv()
        keep_q(r).wait()
        all_peers(r, q_send.at[r], q_recv.at[r]).wait_recv()
        attend(r)
        keep_o(r).start()
        for peer in peers:
            remote(q_buf.at[r, peer], o_buf.at[r, my_rows, my_lanes], o_send.at[r], o_recv.at[r], {'cp': peer}).start()

        @pl.when(r == 0)
        def _():
            hidden.wait()

        @pl.when(r > 0)
        def _():
            project_out(r - 1)

    project_out(n_rounds - 1)
    for r in range(n_rounds):
        share_kv(r).wait_send()
        all_peers(r, q_send.at[r], q_recv.at[r]).wait_send()
        all_peers(r, o_send.at[r], o_recv.at[r]).wait_send()
        pltpu.make_async_copy(x_buf.at[r], y_hbm.at[r], y_sem.at[r]).wait()


def attend(queries, kv_mine, hidden, w_o, n_heads):
    n_rounds, n_dev, tok, head_dim = queries.shape
    rows, width = hidden.shape[1:]
    blk = 4 * tok
    dma = pltpu.SemaphoreType.DMA
    return pl.pallas_call(
        functools.partial(attend_kernel, blk, n_heads),
        out_shape=jax.ShapeDtypeStruct(hidden.shape, hidden.dtype),
        in_specs=[pl.BlockSpec(memory_space=pl.ANY)] * 4,
        out_specs=pl.BlockSpec(memory_space=pl.ANY),
        scratch_shapes=[
            pltpu.VMEM((n_rounds, n_dev, tok, head_dim), jnp.bfloat16),
            pltpu.VMEM((n_rounds, 2, n_dev, tok, head_dim), jnp.bfloat16),
            pltpu.VMEM((n_rounds, rows, n_heads * head_dim), jnp.bfloat16),
            pltpu.VMEM((n_rounds, rows, width), jnp.bfloat16),
            pltpu.VMEM((4, w_o.shape[0], 512), jnp.bfloat16),
            dma((4,)),
            dma,
        ] + [dma((n_rounds,))] * 10,
        compiler_params=pltpu.CompilerParams(collective_id=0, has_side_effects=True, vmem_limit_bytes=66 * 1000 * 1000),
        cost_estimate=pl.CostEstimate(flops=10 ** 11, bytes_accessed=10 ** 8, transcendentals=10 ** 7),
        name='attend',
    )(queries, kv_mine, hidden, w_o)


def solution(mesh):
    cp_size = mesh.shape['cp']

    def per_device(hidden, positions, w_q, w_k, w_v, w_o):
        n_seq, tok_dev, width = hidden.shape
        n_heads, head_dim = w_q.shape[1], w_q.shape[2]
        n_kv = w_k.shape[1]
        per_round = cp_size // n_heads
        n_rounds = n_seq // per_round
        cos_tab, sin_tab = rope_tables(positions, head_dim)
        k_rot = rope_apply(project(hidden, w_k), cos_tab, sin_tab)
        values = project(hidden, w_v)
        kv_all = jnp.stack([k_rot, values]).reshape(2, n_rounds, per_round, tok_dev, n_kv, head_dim)
        kv_send = kv_all.transpose(2, 4, 0, 1, 3, 5).reshape(cp_size, n_rounds, tok_dev, head_dim)
        kv_mine = lax.all_to_all(kv_send, 'cp', 0, 0)
        late, _ = lax.optimization_barrier((hidden, kv_send))
        queries = rope_apply(project(late, w_q), cos_tab, sin_tab)
        queries = queries.transpose(0, 2, 1, 3).reshape(n_rounds, cp_size, tok_dev, head_dim)
        rows = per_round * tok_dev
        out = attend(queries, kv_mine, hidden.reshape(n_rounds, rows, width), w_o.reshape(n_heads * head_dim, width), n_heads)
        return out.reshape(n_seq, tok_dev, width)

    rep_spec = P(None, None, None)
    return jax.shard_map(per_device, mesh=mesh, in_specs=(P('dp', 'cp', None), P('dp', 'cp'), rep_spec, rep_spec, rep_spec, rep_spec), out_specs=P('dp', 'cp', None), check_vma=False)
```

time: 321 us -> 241 us (0.75)
  the two profiles are of different devices: /device:TPU:97 before, /device:TPU:98 now
where the time goes in v2:
time: 241 us; the launch traced here: 240 us
  Pallas kernels  132 us (55%)
  matrix products  47 us (20%)
  waiting for transfers between devices  32.9 us (14%)
  other arithmetic  12.3 us (5%)
  local copies, waits for them, and re-layouts  8.18 us (3%)
  starting transfers between devices  8.13 us (3%)
    pallas_call x1, Pallas kernels, attend(): pl.pallas_call(functools.partial(attend_kernel, blk, n_heads), out_shape=...  132 us
    dot_general x3, matrix products, project(): jnp.einsum('bsd,dhe->bshe', hidden, weights, preferred_element_type=jnp.f...  47 us
    all_to_all x1, waiting for transfers between devices, per_device(): kv_mine = lax.all_to_all(kv_send, 'cp', 0, 0)  32.9 us
    all_to_all x1, starting transfers between devices, per_device(): kv_mine = lax.all_to_all(kv_send, 'cp', 0, 0)  8.13 us
    convert_element_type x2, other arithmetic, rope_apply(): return (val_f32 * cos_tab + rotated * sin_tab).astype(jnp.bfloat16)  6.13 us
    unnamed x17, local copies, waits for them, and re-layouts  5.51 us
  transfers between devices with their start and end apart: 1, of which 1 were waited for; matrix products, arithmetic and copies ran while one was open for 12% of the time, Pallas kernels for 0%

profile of v2, /device:TPU:98, one launch (start us, length us, event | category | flops | bytes accessed | tf_op | source)
XLA Modules:
  0.0 240.4 jit_solution(1634918923482240353)
XLA Ops:
  0.0 0.7 convert_element_type.26
  0.7 0.1 broadcast_multiply_fusion
  0.9 0.0 slice-start
  0.9 2.9 %fusion.30 = (f32[6,96,256]{2,1,0:T(8,128)S(1)}, f32[6,96,256]{2,1,0:T(8,128)}) fusion(f32[6,96,128]{2,1,0:T(8,128)S(1)} %broadcast_multiply_fusion), kind=kLoop, calls=%fused_computation.26 | loop fusion | flops 147456 | bytes 1474560 | tf_op jit(solution)/shard_map/cos | solution.py:19
  3.8 0.0 copy-start.1
  3.8 0.0 copy-start
  3.8 0.0 slice-start.1
  3.8 0.0 slice-start.2
  3.8 0.0 slice-start.3
  3.8 16.1 %fusion.24 = bf16[6,96,8,256]{3,1,2,0:T(8,128)(2,1)} fusion(bf16[3584,8,256]{2,1,0:T(8,128)(2,1)} %param.10, bf16[6,96,3584]{2,1,0:T(8,128)(2,1)} %param.6), kind=kOutput, calls=%fused_computation.23 | convolution fusion | flops 8456896512 | bytes 21168128 | tf_op jit(solution)/shard_map/bsd,dhe->bshe/dot_general | solution.py:30
  19.9 0.0 slice-done
  19.9 0.0 copy-done
  19.9 0.0 slice-done.1
  19.9 0.0 slice-done.2
  19.9 0.0 slice-done.3
  19.9 8.7 %convert_convert_fusion.1 = f32[6,96,8,256]{3,1,2,0:T(8,128)S(1)} fusion(bf16[3584,8,256]{2,1,0:T(8,128)(2,1)S(1)} %bitcast.47, bf16[6,96,3584]{2,1,0:T(8,128)(2,1)S(1)} %copy-done), kind=kOutput, calls=%fused_computation.22 | convolution fusion | flops 8458076160 | bytes 23527424 | tf_op jit(solution)/shard_map/bsd,dhe->bshe/dot_general | solution.py:30
  28.6 0.0 copy-start.2
  28.6 0.6 slice_negate_fusion.1
  29.3 0.0 copy-done.1
  29.3 0.4 copy-done.2
  29.7 0.0 copy-start.3
  29.7 1.1 fusion.12
  30.8 0.5 copy-done.3
  31.3 0.4 pad_maximum_fusion
  31.8 2.7 %copy.14 = bf16[2,3,2,96,8,256]{5,3,1,0,4,2:T(8,128)(2,1)} copy(bf16[2,3,2,96,8,256]{5,3,4,2,1,0:T(8,128)(2,1)S(1)} %pad_maximum_fusion) | data formatting | bytes 9437184 | tf_op jit(solution)/shard_map/stack | solution.py:212
  34.4 8.1 %all-to-all-start = ((bf16[32,3,96,256]{3,2,1,0:T(8,128)(2,1)}), bf16[32,3,96,256]{3,2,1,0:T(8,128)(2,1)}, u32[]{:S(2)}, u32[]{:S(2)}) async-start(bf16[32,3,96,256]{3,2,1,0:T(8,128)(2,1)} %bitcast.45), calls=%async_computation | async-start | bytes 9437184 | tf_op jit(solution)/shard_map/all_to_all | solution.py:214
  42.6 22.3 %convert_convert_fusion = f32[6,96,16,256]{3,1,2,0:T(8,128)S(1)} fusion(bf16[3584,16,256]{2,1,0:T(8,128)(2,1)} %param.8, bf16[6,96,3584]{2,1,0:T(8,128)(2,1)} %param.6), kind=kOutput, calls=%fused_computation.17 | convolution fusion | flops 16916152320 | bytes 42926080 | tf_op jit(solution)/shard_map/bsd,dhe->bshe/dot_general | solution.py:30
  64.9 1.3 slice_negate_fusion
  66.2 5.0 %fusion.10 = bf16[6,96,16,256]{3,1,2,0:T(8,128)(2,1)} fusion(f32[6,96,16,128]{3,1,2,0:T(8,128)S(1)} %get-tuple-element.8, f32[6,96,16,128]{3,1,2,0:T(8,128)S(1)} %get-tuple-element.7, f32[6,96,16,256]{3,1,2,0:T(8,128)S(1)} %convert_convert_fusion, f32[6,96,256]{2,1,0:T(8,128)} %get-tuple-element.12, f32[6,96,256]{2,1,0:T(8,128)} %copy-done.1), kind=kLoop, calls=%fused_computation.11 | loop fusion | flops 11796480 | bytes 24772608 | tf_op jit(solution)/shard_map/convert_element_type | solution.py:26
  71.2 32.9 %all-to-all-done.kv_hbm = bf16[32,3,96,256]{3,2,1,0:T(8,128)(2,1)} async-done(((bf16[32,3,96,256]{3,2,1,0:T(8,128)(2,1)}), bf16[32,3,96,256]{3,2,1,0:T(8,128)(2,1)}, u32[]{:S(2)}, u32[]{:S(2)}) %all-to-all-start) | async-done | bytes 4718624 | tf_op jit(solution)/shard_map/all_to_all | solution.py:214
  104.1 131.7 %attend.1 = bf16[3,192,3584]{2,1,0:T(8,128)(2,1)} custom-call(bf16[3,32,96,256]{3,2,1,0:T(8,128)(2,1)} %bitcast.49, bf16[32,3,96,256]{3,2,1,0:T(8,128)(2,1)} %all-to-all-done.kv_hbm, bf16[3,192,3584]{2,1,0:T(8,128)(2,1)} %bitcast.44, bf16[4096,3584]{1,0:T(8,128)(2,1)} %bitcast.52), custom_call_target="tpu_custom_call" | custom-call | flops 99999997952 | bytes 100000000 | tf_op jit(solution)/shard_map/attend/pallas_call | solution.py:180
  235.8 4.6 %copy.34 = bf16[6,96,3584]{2,1,0:T(8,128)(2,1)} copy(bf16[6,96,3584]{2,1,0:T(8,128)(2,1)} %bitcast.50) | data formatting | bytes 8257536
  (2 shorter events, 0.0 us)
Async XLA Ops:
  0.9 19.0 %slice-start = ((s8[14680064]{0:T(1024)(128)(4,1)}), s8[4194304]{0:T(1024)(128)(4,1)S(1)}, s32[]{:S(2)}) async-start(s8[14680064]{0:T(1024)(128)(4,1)} %bitcast.46), calls=%async_computation.1 | async-start | bytes 8388608
  3.8 25.5 %copy-start.1 = (f32[6,96,256]{2,1,0:T(8,128)}, f32[6,96,256]{2,1,0:T(8,128)S(1)}, u32[]{:S(2)}) copy-start(f32[6,96,256]{2,1,0:T(8,128)S(1)} %get-tuple-element.11) | copy-start | bytes 1769476
  3.8 16.1 %copy-start = (bf16[6,96,3584]{2,1,0:T(8,128)(2,1)S(1)}, bf16[6,96,3584]{2,1,0:T(8,128)(2,1)}, u32[]{:S(2)}) copy-start(bf16[6,96,3584]{2,1,0:T(8,128)(2,1)} %param.6) | copy-start | bytes 12386308
  3.8 16.1 %slice-start.1 = ((s8[14680064]{0:T(1024)(128)(4,1)}), s8[4194304]{0:T(1024)(128)(4,1)S(1)}, s32[]{:S(2)}) async-start(s8[14680064]{0:T(1024)(128)(4,1)} %bitcast.46), calls=%async_computation.2 | async-start | bytes 8388608
  3.8 16.1 %slice-start.2 = ((s8[14680064]{0:T(1024)(128)(4,1)}), s8[4194304]{0:T(1024)(128)(4,1)S(1)}, s32[]{:S(2)}) async-start(s8[14680064]{0:T(1024)(128)(4,1)} %bitcast.46), calls=%async_computation.3 | async-start | bytes 8388608
  3.8 16.1 %slice-start.3 = ((s8[14680064]{0:T(1024)(128)(4,1)}), s8[2097152]{0:T(1024)(128)(4,1)S(1)}, s32[]{:S(2)}) async-start(s8[14680064]{0:T(1024)(128)(4,1)} %bitcast.46), calls=%async_computation.4 | async-start | bytes 4194304
  28.6 1.1 copy-start.2
  29.7 1.7 copy-start.3
  34.4 69.6 %all-to-all-start = ((bf16[32,3,96,256]{3,2,1,0:T(8,128)(2,1)}), bf16[32,3,96,256]{3,2,1,0:T(8,128)(2,1)}, u32[]{:S(2)}, u32[]{:S(2)}) async-start(bf16[32,3,96,256]{3,2,1,0:T(8,128)(2,1)} %bitcast.45), calls=%async_computation | async-start | bytes 9437184 | tf_op jit(solution)/shard_map/all_to_all | solution.py:214

commit v3 on v2

--- a/solution.py
+++ b/solution.py
@@ -38,11 +38,11 @@
                 for a, b in ((dy, dx), (-dy % side, -dx % side), (dx, dy), (-dx % side, -dy % side)):
                     if (a, b, dc) != (0, 0, 0) and (a, b, dc) not in order:
                         order.append((a, b, dc))
-    return order
+    return sorted(order, key=lambda t: -(min(t[0], side - t[0]) + min(t[1], side - t[1])))
 
 
 def attend_kernel(
-    blk, n_heads, q_hbm, kv_hbm, x_hbm, w_hbm, y_hbm, q_buf, kv_buf, o_buf, x_buf, w_buf,
+    blk, n_heads, q_hbm, k_hbm, v_hbm, x_hbm, w_hbm, y_hbm, q_buf, kv_buf, o_buf, x_buf, w_buf,
     w_sem, x_sem, y_sem, q_own, q_send, q_recv, kv_own, kv_send, kv_recv, o_own, o_send, o_recv,
 ):
     n_rounds, n_dev, tok, head_dim = q_buf.shape
@@ -72,11 +72,15 @@
         pl.semaphore_signal(barrier, inc=1, device_id={'cp': peer}, device_id_type=pl.DeviceIdType.MESH)
     hidden = pltpu.make_async_copy(x_hbm, x_buf, x_sem)
 
-    def keep_kv(r):
-        return pltpu.make_async_copy(kv_hbm.at[:, r], kv_buf.at[r, core], kv_own.at[r])
-
-    def share_kv(r):
-        return remote(kv_hbm.at[:, r], kv_buf.at[r, core], kv_send.at[r], kv_recv.at[r], partner)
+    half = pl.ds(pl.multiple_of(core * (tok // 2), tok // 2), tok // 2)
+    kv_hbm = (k_hbm, v_hbm)
+
+    def keep_kv(r, a):
+        return pltpu.make_async_copy(kv_hbm[a].at[:, r], kv_buf.at[r, a, :, half], kv_own.at[2 * r + a])
+
+    def share_kv(r, a):
+        sems = kv_send.at[2 * r + a], kv_recv.at[2 * r + a]
+        return remote(kv_hbm[a].at[:, r], kv_buf.at[r, a, :, half], *sems, partner)
 
     def keep_q(r):
         return pltpu.make_async_copy(q_hbm.at[r, me], q_buf.at[r, me], q_own.at[r])
@@ -88,11 +92,13 @@
         return pltpu.make_async_copy(q_buf.at[r, me], o_buf.at[r, my_rows, my_lanes], o_own.at[r])
 
     for r in range(n_rounds):
-        keep_kv(r).start()
+        for a in range(2):
+            keep_kv(r, a).start()
         keep_q(r).start()
     pl.semaphore_wait(barrier, n_dev - 1)
     for r in range(n_rounds):
-        share_kv(r).start()
+        for a in range(2):
+            share_kv(r, a).start()
         for peer in peers:
             remote(q_hbm.at[r, peer], q_buf.at[r, me], q_send.at[r], q_recv.at[r], {'cp': peer}).start()
     hidden.start()
@@ -147,8 +153,9 @@
 
     @pl.loop(0, n_rounds)
     def _(r):
-        keep_kv(r).wait()
-        share_kv(r).wait_recv()
+        for a in range(2):
+            keep_kv(r, a).wait()
+            share_kv(r, a).wait_recv()
         keep_q(r).wait()
         all_peers(r, q_send.at[r], q_recv.at[r]).wait_recv()
         attend(r)
@@ -166,13 +173,14 @@
 
     project_out(n_rounds - 1)
     for r in range(n_rounds):
-        share_kv(r).wait_send()
+        for a in range(2):
+            share_kv(r, a).wait_send()
         all_peers(r, q_send.at[r], q_recv.at[r]).wait_send()
         all_peers(r, o_send.at[r], o_recv.at[r]).wait_send()
         pltpu.make_async_copy(x_buf.at[r], y_hbm.at[r], y_sem.at[r]).wait()
 
 
-def attend(queries, kv_mine, hidden, w_o, n_heads):
+def attend(queries, k_mine, v_mine, hidden, w_o, n_heads):
     n_rounds, n_dev, tok, head_dim = queries.shape
     rows, width = hidden.shape[1:]
     blk = 4 * tok
@@ -180,7 +188,7 @@
     return pl.pallas_call(
         functools.partial(attend_kernel, blk, n_heads),
         out_shape=jax.ShapeDtypeStruct(hidden.shape, hidden.dtype),
-        in_specs=[pl.BlockSpec(memory_space=pl.ANY)] * 4,
+        in_specs=[pl.BlockSpec(memory_space=pl.ANY)] * 5,
         out_specs=pl.BlockSpec(memory_space=pl.ANY),
         scratch_shapes=[
             pltpu.VMEM((n_rounds, n_dev, tok, head_dim), jnp.bfloat16),
@@ -190,11 +198,11 @@
             pltpu.VMEM((4, w_o.shape[0], 512), jnp.bfloat16),
             dma((4,)),
             dma,
-        ] + [dma((n_rounds,))] * 10,
+        ] + [dma((n_rounds,))] * 4 + [dma((2 * n_rounds,))] * 3 + [dma((n_rounds,))] * 3,
         compiler_params=pltpu.CompilerParams(collective_id=0, has_side_effects=True, vmem_limit_bytes=66 * 1000 * 1000),
         cost_estimate=pl.CostEstimate(flops=10 ** 11, bytes_accessed=10 ** 8, transcendentals=10 ** 7),
         name='attend',
-    )(queries, kv_mine, hidden, w_o)
+    )(queries, k_mine, v_mine, hidden, w_o)
 
 
 def solution(mesh):
@@ -207,16 +215,20 @@
         per_round = cp_size // n_heads
         n_rounds = n_seq // per_round
         cos_tab, sin_tab = rope_tables(positions, head_dim)
-        k_rot = rope_apply(project(hidden, w_k), cos_tab, sin_tab)
-        values = project(hidden, w_v)
-        kv_all = jnp.stack([k_rot, values]).reshape(2, n_rounds, per_round, tok_dev, n_kv, head_dim)
-        kv_send = kv_all.transpose(2, 4, 0, 1, 3, 5).reshape(cp_size, n_rounds, tok_dev, head_dim)
-        kv_mine = lax.all_to_all(kv_send, 'cp', 0, 0)
-        late, _ = lax.optimization_barrier((hidden, kv_send))
+
+        def exchange_halves(heads):
+            parts = heads.reshape(n_rounds, per_round, 2, tok_dev // 2, n_kv, head_dim)
+            send = parts.transpose(1, 4, 2, 0, 3, 5).reshape(cp_size, n_rounds, tok_dev // 2, head_dim)
+            return send, lax.all_to_all(send, 'cp', 0, 0)
+
+        v_send, v_mine = exchange_halves(project(hidden, w_v))
+        late, _ = lax.optimization_barrier((hidden, v_send))
+        k_send, k_mine = exchange_halves(rope_apply(project(late, w_k), cos_tab, sin_tab))
+        late, _ = lax.optimization_barrier((hidden, k_send))
         queries = rope_apply(project(late, w_q), cos_tab, sin_tab)
         queries = queries.transpose(0, 2, 1, 3).reshape(n_rounds, cp_size, tok_dev, head_dim)
         rows = per_round * tok_dev
-        out = attend(queries, kv_mine, hidden.reshape(n_rounds, rows, width), w_o.reshape(n_heads * head_dim, width), n_heads)
+        out = attend(queries, k_mine, v_mine, hidden.reshape(n_rounds, rows, width), w_o.reshape(n_heads * head_dim, width), n_heads)
         return out.reshape(n_seq, tok_dev, width)
 
     rep_spec = P(None, None, None)

time: 241 us -> 229 us (0.950)
  waiting for transfers between devices: 32.9 us -> 17.1 us
  starting transfers between devices: 8.13 us -> 12.1 us
    all_to_all x1 -> x2, waiting for transfers between devices: 32.9 us -> 17.1 us  [exchange_halves(): return (send, lax.all_to_all(send, 'cp', 0, 0))]
    all_to_all x1 -> x2, starting transfers between devices: 8.13 us -> 12.1 us  [exchange_halves(): return (send, lax.all_to_all(send, 'cp', 0, 0))]
    reshape x0 -> x2, local copies, waits for them, and re-layouts: none -> 3.12 us  [exchange_halves(): parts = heads.reshape(n_rounds, per_round, 2, tok_dev // 2, n_kv, head_dim)]
    another operation x1 -> x0, local copies, waits for them, and re-layouts: 2.67 us -> none  [per_device(): jnp.stack([k_rot, values])]
    unnamed x17 -> x9, local copies, waits for them, and re-layouts: 5.51 us -> 5 us
  transfers between devices with their start and end apart: 1 -> 2, of which waited for: 1 -> 2; matrix products, arithmetic and copies ran while one was open for 12% -> 21% of each run, Pallas kernels for 0% -> 0%
where the time goes in v3:
time: 229 us; the launch traced here: 228 us
  Pallas kernels  132 us (58%)
  matrix products  48.8 us (21%)
  waiting for transfers between devices  17.1 us (7%)
  starting transfers between devices  12.1 us (5%)
  other arithmetic  10.2 us (4%)
  local copies, waits for them, and re-layouts  8.12 us (4%)
    pallas_call x1, Pallas kernels, attend(): pl.pallas_call(functools.partial(attend_kernel, blk, n_heads), out_shape=...  132 us
    dot_general x3, matrix products, project(): jnp.einsum('bsd,dhe->bshe', hidden, weights, preferred_element_type=jnp.f...  48.8 us
    all_to_all x2, waiting for transfers between devices, exchange_halves(): return (send, lax.all_to_all(send, 'cp', 0, 0))  17.1 us
    all_to_all x2, starting transfers between devices, exchange_halves(): return (send, lax.all_to_all(send, 'cp', 0, 0))  12.1 us
    convert_element_type x2, other arithmetic, rope_apply(): return (val_f32 * cos_tab + rotated * sin_tab).astype(jnp.bfloat16)  6.05 us
    unnamed x9, local copies, waits for them, and re-layouts  5 us
  transfers between devices with their start and end apart: 2, of which 2 were waited for; matrix products, arithmetic and copies ran while one was open for 21% of the time, Pallas kernels for 0%

profile of v3, /device:TPU:98, one launch (start us, length us, event | category | flops | bytes accessed | tf_op | source)
XLA Modules:
  0.0 228.5 jit_solution(2537733217452638107)
XLA Ops:
  0.0 13.2 %fusion.20 = bf16[6,96,8,256]{3,1,2,0:T(8,128)(2,1)S(1)} fusion(bf16[3584,8,256]{2,1,0:T(8,128)(2,1)} %param.10, bf16[6,96,3584]{2,1,0:T(8,128)(2,1)} %param.6), kind=kOutput, calls=%fused_computation.22 | convolution fusion | flops 8456896512 | bytes 21168128 | tf_op jit(solution)/shard_map/bsd,dhe->bshe/dot_general | solution.py:30
  13.3 1.6 copy.8
  14.8 8.1 %all-to-all-start.1 = ((bf16[32,3,48,256]{3,2,1,0:T(8,128)(2,1)}), bf16[32,3,48,256]{3,2,1,0:T(8,128)(2,1)S(1)}, u32[]{:S(2)}, u32[]{:S(2)}) async-start(bf16[32,3,48,256]{3,2,1,0:T(8,128)(2,1)} %bitcast.5), calls=%async_computation.1 | async-start | bytes 4718592 | tf_op jit(solution)/shard_map/all_to_all | solution.py:222
  22.9 0.0 copy-start.3
  22.9 13.3 %convert_convert_fusion.1 = f32[6,96,8,256]{3,1,2,0:T(8,128)S(1)} fusion(bf16[3584,8,256]{2,1,0:T(8,128)(2,1)} %param.9, bf16[6,96,3584]{2,1,0:T(8,128)(2,1)} %param.6), kind=kOutput, calls=%fused_computation.21 | convolution fusion | flops 8458076160 | bytes 23527424 | tf_op jit(solution)/shard_map/bsd,dhe->bshe/dot_general | solution.py:30
  36.2 0.0 copy-done.3
  36.3 0.1 broadcast_multiply_fusion
  36.4 2.1 fusion.30
  38.5 0.0 copy-start
  38.5 0.0 copy-start.1
  38.5 0.6 slice_negate_fusion.1
  39.2 0.2 copy-done
  39.4 0.2 copy-done.1
  39.6 1.1 fusion.12
  40.7 1.6 copy.10
  42.3 13.4 %all-to-all-done.1.v_hbm = bf16[32,3,48,256]{3,2,1,0:T(8,128)(2,1)S(1)} async-done(((bf16[32,3,48,256]{3,2,1,0:T(8,128)(2,1)}), bf16[32,3,48,256]{3,2,1,0:T(8,128)(2,1)S(1)}, u32[]{:S(2)}, u32[]{:S(2)}) %all-to-all-start.1) | async-done | bytes 2359328 | tf_op jit(solution)/shard_map/all_to_all | solution.py:222
  55.7 0.0 copy-start.2
  55.7 4.0 %all-to-all-start = ((bf16[32,3,48,256]{3,2,1,0:T(8,128)(2,1)}), bf16[32,3,48,256]{3,2,1,0:T(8,128)(2,1)}, u32[]{:S(2)}, u32[]{:S(2)}) async-start(bf16[32,3,48,256]{3,2,1,0:T(8,128)(2,1)} %bitcast.11), calls=%async_computation | async-start | bytes 4718592 | tf_op jit(solution)/shard_map/all_to_all | solution.py:222
  59.7 0.0 copy-done.2
  59.7 22.3 %convert_convert_fusion = f32[6,96,16,256]{3,1,2,0:T(8,128)S(1)} fusion(bf16[3584,16,256]{2,1,0:T(8,128)(2,1)} %param.8, bf16[6,96,3584]{2,1,0:T(8,128)(2,1)} %param.6), kind=kOutput, calls=%fused_computation.16 | convolution fusion | flops 16916152320 | bytes 42926080 | tf_op jit(solution)/shard_map/bsd,dhe->bshe/dot_general | solution.py:30
  82.0 1.3 slice_negate_fusion
  83.3 4.9 %fusion.10 = bf16[6,96,16,256]{3,1,2,0:T(8,128)(2,1)} fusion(f32[6,96,16,128]{3,1,2,0:T(8,128)S(1)} %get-tuple-element.10, f32[6,96,16,128]{3,1,2,0:T(8,128)S(1)} %get-tuple-element.9, f32[6,96,16,256]{3,1,2,0:T(8,128)S(1)} %convert_convert_fusion, f32[6,96,256]{2,1,0:T(8,128)} %copy-done.1, f32[6,96,256]{2,1,0:T(8,128)} %copy-done), kind=kLoop, calls=%fused_computation.11 | loop fusion | flops 11796480 | bytes 24772608 | tf_op jit(solution)/shard_map/convert_element_type | solution.py:26
  88.2 3.8 %all-to-all-done.k_hbm = bf16[32,3,48,256]{3,2,1,0:T(8,128)(2,1)} async-done(((bf16[32,3,48,256]{3,2,1,0:T(8,128)(2,1)}), bf16[32,3,48,256]{3,2,1,0:T(8,128)(2,1)}, u32[]{:S(2)}, u32[]{:S(2)}) %all-to-all-start) | async-done | bytes 2359328 | tf_op jit(solution)/shard_map/all_to_all | solution.py:222
  91.9 132.0 %attend.1 = bf16[3,192,3584]{2,1,0:T(8,128)(2,1)} custom-call(bf16[3,32,96,256]{3,2,1,0:T(8,128)(2,1)} %bitcast.52, bf16[32,3,48,256]{3,2,1,0:T(8,128)(2,1)} %all-to-all-done.k_hbm, bf16[32,3,48,256]{3,2,1,0:T(8,128)(2,1)} %copy-done.2, bf16[3,192,3584]{2,1,0:T(8,128)(2,1)} %bitcast.50, bf16[4096,3584]{1,0:T(8,128)(2,1)} %bitcast.55), custom_call_target="tpu_custom_call" | custom-call | flops 99999997952 | bytes 100000000 | tf_op jit(solution)/shard_map/attend/pallas_call | solution.py:188
  223.9 4.6 %copy.34 = bf16[6,96,3584]{2,1,0:T(8,128)(2,1)} copy(bf16[6,96,3584]{2,1,0:T(8,128)(2,1)} %bitcast.53) | data formatting | bytes 8257536
  (2 shorter events, 0.0 us)
Async XLA Ops:
  14.8 40.8 %all-to-all-start.1 = ((bf16[32,3,48,256]{3,2,1,0:T(8,128)(2,1)}), bf16[32,3,48,256]{3,2,1,0:T(8,128)(2,1)S(1)}, u32[]{:S(2)}, u32[]{:S(2)}) async-start(bf16[32,3,48,256]{3,2,1,0:T(8,128)(2,1)} %bitcast.5), calls=%async_computation.1 | async-start | bytes 4718592 | tf_op jit(solution)/shard_map/all_to_all | solution.py:222
  22.9 13.3 %copy-start.3 = (s32[6,96]{1,0:T(8,128)S(1)}, s32[6,96]{1,0:T(8,128)}, u32[]{:S(2)}) copy-start(s32[6,96]{1,0:T(8,128)} %param.7) | copy-start | bytes 6916
  38.5 0.9 copy-start
  38.5 1.1 copy-start.1
  55.7 4.0 %copy-start.2 = (bf16[32,3,48,256]{3,2,1,0:T(8,128)(2,1)}, bf16[32,3,48,256]{3,2,1,0:T(8,128)(2,1)S(1)}, u32[]{:S(2)}) copy-start(bf16[32,3,48,256]{3,2,1,0:T(8,128)(2,1)S(1)} %all-to-all-done.1.v_hbm) | copy-start | bytes 7077892
  55.7 36.3 %all-to-all-start = ((bf16[32,3,48,256]{3,2,1,0:T(8,128)(2,1)}), bf16[32,3,48,256]{3,2,1,0:T(8,128)(2,1)}, u32[]{:S(2)}, u32[]{:S(2)}) async-start(bf16[32,3,48,256]{3,2,1,0:T(8,128)(2,1)} %bitcast.11), calls=%async_computation | async-start | bytes 4718592 | tf_op jit(solution)/shard_map/all_to_all | solution.py:222

commit v4 on v3

--- a/solution.py
+++ b/solution.py
@@ -151,6 +151,11 @@
 
         pltpu.make_async_copy(x_buf.at[r], y_hbm.at[r], y_sem.at[r]).start()
 
+    def send_o(r):
+        keep_o(r).start()
+        for peer in peers:
+            remote(q_buf.at[r, peer], o_buf.at[r, my_rows, my_lanes], o_send.at[r], o_recv.at[r], {'cp': peer}).start()
+
     @pl.loop(0, n_rounds)
     def _(r):
         for a in range(2):
@@ -159,23 +164,23 @@
         keep_q(r).wait()
         all_peers(r, q_send.at[r], q_recv.at[r]).wait_recv()
         attend(r)
-        keep_o(r).start()
-        for peer in peers:
-            remote(q_buf.at[r, peer], o_buf.at[r, my_rows, my_lanes], o_send.at[r], o_recv.at[r], {'cp': peer}).start()
-
-        @pl.when(r == 0)
+
+        @pl.when(r == n_rounds - 2)
         def _():
-            hidden.wait()
-
-        @pl.when(r > 0)
+            for q in range(n_rounds):
+                all_peers(q, q_send.at[q], q_recv.at[q]).wait_send()
+            for q in range(n_rounds - 1):
+                send_o(q)
+
+        @pl.when(r == n_rounds - 1)
         def _():
-            project_out(r - 1)
-
-    project_out(n_rounds - 1)
+            send_o(r)
+
+    hidden.wait()
+    pl.loop(0, n_rounds)(project_out)
     for r in range(n_rounds):
         for a in range(2):
             share_kv(r, a).wait_send()
-        all_peers(r, q_send.at[r], q_recv.at[r]).wait_send()
         all_peers(r, o_send.at[r], o_recv.at[r]).wait_send()
         pltpu.make_async_copy(x_buf.at[r], y_hbm.at[r], y_sem.at[r]).wait()
 

time: 229 us -> 227 us (level)
  Pallas kernels: 132 us -> 128 us
    pallas_call x1, Pallas kernels: 132 us -> 128 us  [attend(): pl.pallas_call(functools.partial(attend_kernel, blk, n_heads), out_shape=...]
where the time goes in v4:
time: 227 us; the launch traced here: 224 us
  Pallas kernels  128 us (56%)
  matrix products  48.8 us (21%)
  waiting for transfers between devices  17.1 us (8%)
  starting transfers between devices  12.1 us (5%)
  other arithmetic  10.2 us (4%)
  local copies, waits for them, and re-layouts  8.12 us (4%)
    pallas_call x1, Pallas kernels, attend(): pl.pallas_call(functools.partial(attend_kernel, blk, n_heads), out_shape=...  128 us
    dot_general x3, matrix products, project(): jnp.einsum('bsd,dhe->bshe', hidden, weights, preferred_element_type=jnp.f...  48.8 us
    all_to_all x2, waiting for transfers between devices, exchange_halves(): return (send, lax.all_to_all(send, 'cp', 0, 0))  17.1 us
    all_to_all x2, starting transfers between devices, exchange_halves(): return (send, lax.all_to_all(send, 'cp', 0, 0))  12.1 us
    convert_element_type x2, other arithmetic, rope_apply(): return (val_f32 * cos_tab + rotated * sin_tab).astype(jnp.bfloat16)  6.05 us
    unnamed x9, local copies, waits for them, and re-layouts  5 us
  transfers between devices with their start and end apart: 2, of which 2 were waited for; matrix products, arithmetic and copies ran while one was open for 21% of the time, Pallas kernels for 0%

profile of v4, /device:TPU:98, one launch (start us, length us, event | category | flops | bytes accessed | tf_op | source)
XLA Modules:
  0.0 224.5 jit_solution(6568782189205259880)
XLA Ops:
  0.0 13.2 %fusion.20 = bf16[6,96,8,256]{3,1,2,0:T(8,128)(2,1)S(1)} fusion(bf16[3584,8,256]{2,1,0:T(8,128)(2,1)} %param.10, bf16[6,96,3584]{2,1,0:T(8,128)(2,1)} %param.6), kind=kOutput, calls=%fused_computation.22 | convolution fusion | flops 8456896512 | bytes 21168128 | tf_op jit(solution)/shard_map/bsd,dhe->bshe/dot_general | solution.py:30
  13.3 1.6 copy.8
  14.8 8.1 %all-to-all-start.1 = ((bf16[32,3,48,256]{3,2,1,0:T(8,128)(2,1)}), bf16[32,3,48,256]{3,2,1,0:T(8,128)(2,1)S(1)}, u32[]{:S(2)}, u32[]{:S(2)}) async-start(bf16[32,3,48,256]{3,2,1,0:T(8,128)(2,1)} %bitcast.5), calls=%async_computation.1 | async-start | bytes 4718592 | tf_op jit(solution)/shard_map/all_to_all | solution.py:227
  22.9 0.0 copy-start.3
  22.9 13.3 %convert_convert_fusion.1 = f32[6,96,8,256]{3,1,2,0:T(8,128)S(1)} fusion(bf16[3584,8,256]{2,1,0:T(8,128)(2,1)} %param.9, bf16[6,96,3584]{2,1,0:T(8,128)(2,1)} %param.6), kind=kOutput, calls=%fused_computation.21 | convolution fusion | flops 8458076160 | bytes 23527424 | tf_op jit(solution)/shard_map/bsd,dhe->bshe/dot_general | solution.py:30
  36.2 0.0 copy-done.3
  36.3 0.1 broadcast_multiply_fusion
  36.4 2.1 fusion.30
  38.5 0.0 copy-start
  38.5 0.0 copy-start.1
  38.5 0.6 slice_negate_fusion.1
  39.2 0.2 copy-done
  39.4 0.2 copy-done.1
  39.6 1.1 fusion.12
  40.7 1.6 copy.10
  42.3 13.4 %all-to-all-done.1.v_hbm = bf16[32,3,48,256]{3,2,1,0:T(8,128)(2,1)S(1)} async-done(((bf16[32,3,48,256]{3,2,1,0:T(8,128)(2,1)}), bf16[32,3,48,256]{3,2,1,0:T(8,128)(2,1)S(1)}, u32[]{:S(2)}, u32[]{:S(2)}) %all-to-all-start.1) | async-done | bytes 2359328 | tf_op jit(solution)/shard_map/all_to_all | solution.py:227
  55.7 0.0 copy-start.2
  55.7 4.0 %all-to-all-start = ((bf16[32,3,48,256]{3,2,1,0:T(8,128)(2,1)}), bf16[32,3,48,256]{3,2,1,0:T(8,128)(2,1)}, u32[]{:S(2)}, u32[]{:S(2)}) async-start(bf16[32,3,48,256]{3,2,1,0:T(8,128)(2,1)} %bitcast.11), calls=%async_computation | async-start | bytes 4718592 | tf_op jit(solution)/shard_map/all_to_all | solution.py:227
  59.7 0.0 copy-done.2
  59.7 22.3 %convert_convert_fusion = f32[6,96,16,256]{3,1,2,0:T(8,128)S(1)} fusion(bf16[3584,16,256]{2,1,0:T(8,128)(2,1)} %param.8, bf16[6,96,3584]{2,1,0:T(8,128)(2,1)} %param.6), kind=kOutput, calls=%fused_computation.16 | convolution fusion | flops 16916152320 | bytes 42926080 | tf_op jit(solution)/shard_map/bsd,dhe->bshe/dot_general | solution.py:30
  82.0 1.3 slice_negate_fusion
  83.3 4.9 %fusion.10 = bf16[6,96,16,256]{3,1,2,0:T(8,128)(2,1)} fusion(f32[6,96,16,128]{3,1,2,0:T(8,128)S(1)} %get-tuple-element.10, f32[6,96,16,128]{3,1,2,0:T(8,128)S(1)} %get-tuple-element.9, f32[6,96,16,256]{3,1,2,0:T(8,128)S(1)} %convert_convert_fusion, f32[6,96,256]{2,1,0:T(8,128)} %copy-done.1, f32[6,96,256]{2,1,0:T(8,128)} %copy-done), kind=kLoop, calls=%fused_computation.11 | loop fusion | flops 11796480 | bytes 24772608 | tf_op jit(solution)/shard_map/convert_element_type | solution.py:26
  88.2 3.8 %all-to-all-done.k_hbm = bf16[32,3,48,256]{3,2,1,0:T(8,128)(2,1)} async-done(((bf16[32,3,48,256]{3,2,1,0:T(8,128)(2,1)}), bf16[32,3,48,256]{3,2,1,0:T(8,128)(2,1)}, u32[]{:S(2)}, u32[]{:S(2)}) %all-to-all-start) | async-done | bytes 2359328 | tf_op jit(solution)/shard_map/all_to_all | solution.py:227
  91.9 128.0 %attend.1 = bf16[3,192,3584]{2,1,0:T(8,128)(2,1)} custom-call(bf16[3,32,96,256]{3,2,1,0:T(8,128)(2,1)} %bitcast.52, bf16[32,3,48,256]{3,2,1,0:T(8,128)(2,1)} %all-to-all-done.k_hbm, bf16[32,3,48,256]{3,2,1,0:T(8,128)(2,1)} %copy-done.2, bf16[3,192,3584]{2,1,0:T(8,128)(2,1)} %bitcast.50, bf16[4096,3584]{1,0:T(8,128)(2,1)} %bitcast.55), custom_call_target="tpu_custom_call" | custom-call | flops 99999997952 | bytes 100000000 | tf_op jit(solution)/shard_map/attend/pallas_call | solution.py:193
  219.9 4.6 %copy.34 = bf16[6,96,3584]{2,1,0:T(8,128)(2,1)} copy(bf16[6,96,3584]{2,1,0:T(8,128)(2,1)} %bitcast.53) | data formatting | bytes 8257536
  (2 shorter events, 0.0 us)
Async XLA Ops:
  14.8 40.8 %all-to-all-start.1 = ((bf16[32,3,48,256]{3,2,1,0:T(8,128)(2,1)}), bf16[32,3,48,256]{3,2,1,0:T(8,128)(2,1)S(1)}, u32[]{:S(2)}, u32[]{:S(2)}) async-start(bf16[32,3,48,256]{3,2,1,0:T(8,128)(2,1)} %bitcast.5), calls=%async_computation.1 | async-start | bytes 4718592 | tf_op jit(solution)/shard_map/all_to_all | solution.py:227
  22.9 13.3 %copy-start.3 = (s32[6,96]{1,0:T(8,128)S(1)}, s32[6,96]{1,0:T(8,128)}, u32[]{:S(2)}) copy-start(s32[6,96]{1,0:T(8,128)} %param.7) | copy-start | bytes 6916
  38.5 0.9 copy-start
  38.5 1.1 copy-start.1
  55.7 4.0 %copy-start.2 = (bf16[32,3,48,256]{3,2,1,0:T(8,128)(2,1)}, bf16[32,3,48,256]{3,2,1,0:T(8,128)(2,1)S(1)}, u32[]{:S(2)}) copy-start(bf16[32,3,48,256]{3,2,1,0:T(8,128)(2,1)S(1)} %all-to-all-done.1.v_hbm) | copy-start | bytes 7077892
  55.7 36.3 %all-to-all-start = ((bf16[32,3,48,256]{3,2,1,0:T(8,128)(2,1)}), bf16[32,3,48,256]{3,2,1,0:T(8,128)(2,1)}, u32[]{:S(2)}, u32[]{:S(2)}) async-start(bf16[32,3,48,256]{3,2,1,0:T(8,128)(2,1)} %bitcast.11), calls=%async_computation | async-start | bytes 4718592 | tf_op jit(solution)/shard_map/all_to_all | solution.py:227
